TPU v7x, 256 devices: a whole 4x4x8 slice. The times are simulated.
256 devices in a mesh: row: 16 (over z, core), col: 16 (over x, y).
Axes of the slice: x: 4, y: 4, z: 8, core: 2. Of those that a mesh axis runs over, the one named last changes fastest.
Arguments:
- attn_out: bfloat16 [6, 4096, 2048], P(None, 'col', 'row'), may hold values from -0.25 to 0.25
- out_cotangent: bfloat16 [6, 4096, 2048], P(None, 'row', 'col'), may hold values from -6 to 6
- frozen: bfloat16 [6, 2048, 2048], P(None, 'row', 'col'), may hold values from -0.5 to 0.5
- adapt_in: bfloat16 [6, 32, 2048], P(None, None, 'row'), may hold values from -0.125 to 0.125
- adapt_out: bfloat16 [6, 32, 2048], P(None, None, 'col'), may hold values from -1 to 1
- magnitude: float32 [6, 2048], P(None, 'col'), may hold values from 0.1 to 1.9
Outputs:
- input_grad: bfloat16 [6, 4096, 2048], P(None, 'col', 'row')
- adapt_in_grad: float32 [6, 32, 2048], P(None, None, 'row')
- adapt_out_grad: float32 [6, 32, 2048], P(None, None, 'col')
- magnitude_grad: float32 [6, 2048], P(None, 'col')
All inputs are finite; a program needn't handle non-finite values.
Results may differ from a plain program's by a relative error of at most 0.0065.
Values may be sent and summed in bfloat16 or wider, within the bound.
A program may use at most 64 MiB of HBM per device.

v0:
```python
import jax
import jax.numpy as jnp
from jax import lax
from jax.sharding import PartitionSpec as P

precise = lax.Precision.HIGHEST


def in_order(pieces, dim):
    pieces = jnp.moveaxis(pieces, 0, dim)
    dims = pieces.shape
    return pieces.reshape(*dims[:dim], dims[dim] * dims[dim + 1], *dims[dim + 2 :])


def from_everyone(shard, axis):
    copies = jnp.broadcast_to(shard, (lax.axis_size(axis), *shard.shape))
    return lax.all_to_all(copies, axis, split_axis=0, concat_axis=0, tiled=True)


def gathered_copies(shard, axis, dim):
    return in_order(from_everyone(shard, axis), dim)


def over_copies(shard, axis):
    everything = from_everyone(shard, axis)
    return jnp.sum(everything, axis=0)


def packed_total(arrays, axis):
    line, at, finished = (jnp.concatenate([a.reshape(-1) for a in arrays]), 0, [])
    subtotal = over_copies(line, axis)
    for a in arrays:
        finished.append(subtotal[at : at + a.size].reshape(a.shape))
        at += a.size
    return tuple(finished)


def cut_along(shard, dim, size):
    dims = shard.shape
    pieces = shard.reshape(*dims[:dim], size, dims[dim] // size, *dims[dim + 1 :])
    return jnp.moveaxis(pieces, dim, 0)


def sum_at_owner(shard, axis, dim):
    pieces = cut_along(shard, dim, lax.axis_size(axis))
    arrived = lax.all_to_all(pieces, axis, split_axis=0, concat_axis=0, tiled=True)
    return arrived.astype(jnp.float32).sum(axis=0)


def one_layer(acts, grads, frozen, adapt_in, adapt_out, magnitude):
    merged = frozen.astype(jnp.float32) + lax.dot_general(
        adapt_in, adapt_out, (((0,), (0,)), ((), ())), preferred_element_type=jnp.float32
    )
    squares_part = jnp.sum(merged * merged, axis=0)
    grads_all = lax.all_gather(grads, "row", axis=0, tiled=True)
    outer = lax.dot_general(
        gathered_copies(acts, "col", 0),
        grads_all,
        (((0,), (0,)), ((), ())),
        preferred_element_type=jnp.float32,
    )
    dots_part = jnp.sum(merged * outer, axis=0)
    adapt_in_wide = adapt_in.astype(jnp.float32)
    inner_outer = jnp.dot(adapt_in_wide, outer, precision=precise)
    inner_merged = jnp.dot(adapt_in_wide, merged, precision=precise)
    squares, dots, inner_outer, inner_merged = packed_total(
        (squares_part, dots_part, inner_outer, inner_merged), "row"
    )
    norms = jnp.sqrt(squares + 0.25)
    scales = magnitude / norms
    correct = -magnitude * dots / (norms * norms * norms)
    delta = outer * scales + merged * correct
    out_grad = inner_outer * scales + inner_merged * correct
    magnitude_grad = dots / norms
    in_part = lax.dot_general(
        adapt_out.astype(jnp.float32), delta, (((1,), (1,)), ((), ())), precision=precise
    )
    in_grad = over_copies(in_part, "col")
    scaled = (grads_all * scales).astype(jnp.bfloat16)
    weight_low = merged.astype(jnp.bfloat16)
    summed = sum_at_owner(
        lax.dot_general(
            scaled, weight_low, (((1,), (1,)), ((), ())), preferred_element_type=jnp.float32
        ).astype(jnp.bfloat16),
        "col",
        0,
    )
    return (summed.astype(jnp.bfloat16), in_grad, out_grad, magnitude_grad)


def body(attn_out, out_cotangent, frozen, adapt_in, adapt_out, magnitude):
    results = [
        one_layer(
            attn_out[layer_at],
            out_cotangent[layer_at],
            frozen[layer_at],
            adapt_in[layer_at],
            adapt_out[layer_at],
            magnitude[layer_at],
        )
        for layer_at in range(frozen.shape[0])
    ]
    return (
        jnp.stack([item[0] for item in results]),
        jnp.stack([item[1] for item in results]),
        jnp.stack([item[2] for item in results]),
        jnp.stack([item[3] for item in results]),
    )


def solution(mesh):
    return jax.shard_map(
        body,
        mesh=mesh,
        in_specs=(
            P(None, "col", "row"),
            P(None, "row", "col"),
            P(None, "row", "col"),
            P(None, None, "row"),
            P(None, None, "col"),
            P(None, "col"),
        ),
        out_specs=(
            P(None, "col", "row"),
            P(None, None, "row"),
            P(None, None, "col"),
            P(None, "col"),
        ),
        check_vma=False,
    )
```

profile of v0, /device:TPU:160, one launch (start us, length us, event | category | flops | bytes accessed | tf_op | source)
XLA Modules:
  0.0 485.4 jit_solution(7138014174976289874)
XLA Ops:
  18.0 17.0 %all-to-all-done = bf16[16,256,128]{2,1,0:T(8,128)(2,1)S(1)} async-done(((bf16[16,256,128]{2,1,0:T(8,128)(2,1)}), bf16[16,256,128]{2,1,0:T(8,128)(2,1)S(1)}, u32[]{:S(2)}, u32[]{:S(2)}) %all-to-all-start) | async-done | bytes 1048608 | tf_op jit(solution)/shard_map/all_to_all | solution.py:17
  35.2 18.8 %all_to_all.126 = bf16[16,256,128]{2,1,0:T(8,128)(2,1)} all-to-all(bf16[16,256,128]{2,1,0:T(8,128)(2,1)S(1)} %broadcast_in_dim.46), channel_id=1, replica_groups=mesh['row'=16,'col'=16] {'col'}, dimensions={0} | all-to-all | bytes 2097152 | tf_op jit(solution)/shard_map/all_to_all | solution.py:17
  59.6 14.0 %all-to-all-done.3 = bf16[16,256,128]{2,1,0:T(8,128)(2,1)S(1)} async-done(((bf16[16,256,128]{2,1,0:T(8,128)(2,1)}), bf16[16,256,128]{2,1,0:T(8,128)(2,1)S(1)}, u32[]{:S(2)}, u32[]{:S(2)}) %all-to-all-start.3) | async-done | bytes 1048608 | tf_op jit(solution)/shard_map/all_to_all | solution.py:17
  73.8 18.9 %all_to_all.127 = bf16[16,256,128]{2,1,0:T(8,128)(2,1)S(1)} all-to-all(bf16[16,256,128]{2,1,0:T(8,128)(2,1)S(1)} %broadcast_in_dim.44), channel_id=1, replica_groups=mesh['row'=16,'col'=16] {'col'}, dimensions={0} | all-to-all | bytes 2097152 | tf_op jit(solution)/shard_map/all_to_all | solution.py:17
  98.3 14.4 %all-to-all-done.6 = bf16[16,256,128]{2,1,0:T(8,128)(2,1)S(1)} async-done(((bf16[16,256,128]{2,1,0:T(8,128)(2,1)}), bf16[16,256,128]{2,1,0:T(8,128)(2,1)S(1)}, u32[]{:S(2)}, u32[]{:S(2)}) %all-to-all-start.6) | async-done | bytes 1048608 | tf_op jit(solution)/shard_map/all_to_all | solution.py:17
  121.0 12.0 %all-to-all-done.9 = bf16[16,256,128]{2,1,0:T(8,128)(2,1)S(1)} async-done(((bf16[16,256,128]{2,1,0:T(8,128)(2,1)}), bf16[16,256,128]{2,1,0:T(8,128)(2,1)S(1)}, u32[]{:S(2)}, u32[]{:S(2)}) %all-to-all-start.9) | async-done | bytes 1048608 | tf_op jit(solution)/shard_map/all_to_all | solution.py:17
  144.8 12.9 %all-to-all-done.1 = f32[16,1,8448]{2,1,0:T(1,128)} async-done(((f32[16,1,8448]{2,1,0:T(1,128)}), f32[16,1,8448]{2,1,0:T(1,128)}, u32[]{:S(2)}, u32[]{:S(2)}) %all-to-all-start.1) | async-done | bytes 540704 | tf_op jit(solution)/shard_map/all_to_all | solution.py:17
  169.2 10.3 %all-to-all-done.16 = f32[16,1,8448]{2,1,0:T(1,128)} async-done(((f32[16,1,8448]{2,1,0:T(1,128)}), f32[16,1,8448]{2,1,0:T(1,128)}, u32[]{:S(2)}, u32[]{:S(2)}) %all-to-all-start.16) | async-done | bytes 540704 | tf_op jit(solution)/shard_map/all_to_all | solution.py:17
  191.4 13.2 %all-to-all-done.4 = f32[16,1,8448]{2,1,0:T(1,128)} async-done(((f32[16,1,8448]{2,1,0:T(1,128)}), f32[16,1,8448]{2,1,0:T(1,128)}, u32[]{:S(2)}, u32[]{:S(2)}) %all-to-all-start.4) | async-done | bytes 540704 | tf_op jit(solution)/shard_map/all_to_all | solution.py:17
  215.2 11.2 %all-to-all-done.13 = f32[16,1,8448]{2,1,0:T(1,128)S(1)} async-done(((f32[16,1,8448]{2,1,0:T(1,128)}), f32[16,1,8448]{2,1,0:T(1,128)S(1)}, u32[]{:S(2)}, u32[]{:S(2)}) %all-to-all-start.13) | async-done | bytes 540704 | tf_op jit(solution)/shard_map/all_to_all | solution.py:17
  233.8 19.4 %all-gather.19.cloned.1.call-done = bf16[1,4096,128]{2,1,0:T(8,128)(2,1)} async-done(((bf16[1,256,128]{2,1,0:T(8,128)(2,1)}), bf16[1,4096,128]{2,1,0:T(8,128)(2,1)}) %all-gather.19.cloned.1.call-update) | async-done | bytes 1048592 | tf_op jit(solution)/shard_map/all_gather | solution.py:55
  257.4 7.5 %all-to-all-start.10 = ((f32[16,1,8448]{2,1,0:T(1,128)}), f32[16,1,8448]{2,1,0:T(1,128)S(1)}, u32[]{:S(2)}, u32[]{:S(2)}) async-start(f32[16,1,8448]{2,1,0:T(1,128)} %broadcast_in_dim.43), calls=%async_computation.10 | async-start | bytes 1081344 | tf_op jit(solution)/shard_map/all_to_all | solution.py:17
  270.2 8.8 %all-to-all-done.10 = f32[16,1,8448]{2,1,0:T(1,128)S(1)} async-done(((f32[16,1,8448]{2,1,0:T(1,128)}), f32[16,1,8448]{2,1,0:T(1,128)S(1)}, u32[]{:S(2)}, u32[]{:S(2)}) %all-to-all-start.10) | async-done | bytes 540704 | tf_op jit(solution)/shard_map/all_to_all | solution.py:17
  279.8 7.3 %all-to-all-start.18 = ((f32[16,32,128]{2,1,0:T(8,128)}), f32[16,32,128]{2,1,0:T(8,128)S(1)}, u32[]{:S(2)}, u32[]{:S(2)}) async-start(f32[16,32,128]{2,1,0:T(8,128)} %broadcast_in_dim.96), calls=%async_computation.18 | async-start | bytes 524288 | tf_op jit(solution)/shard_map/all_to_all | solution.py:17
  300.7 7.8 %all-to-all-done.19 = f32[16,32,128]{2,1,0:T(8,128)S(1)} async-done(((f32[16,32,128]{2,1,0:T(8,128)}), f32[16,32,128]{2,1,0:T(8,128)S(1)}, u32[]{:S(2)}, u32[]{:S(2)}) %all-to-all-start.19) | async-done | bytes 262176 | tf_op jit(solution)/shard_map/all_to_all | solution.py:17
  313.1 8.3 %all-to-all-done.20 = f32[16,32,128]{2,1,0:T(8,128)S(1)} async-done(((f32[16,32,128]{2,1,0:T(8,128)}), f32[16,32,128]{2,1,0:T(8,128)S(1)}, u32[]{:S(2)}, u32[]{:S(2)}) %all-to-all-start.20) | async-done | bytes 262176 | tf_op jit(solution)/shard_map/all_to_all | solution.py:17
  326.1 8.3 %all-to-all-done.21 = f32[16,32,128]{2,1,0:T(8,128)S(1)} async-done(((f32[16,32,128]{2,1,0:T(8,128)}), f32[16,32,128]{2,1,0:T(8,128)S(1)}, u32[]{:S(2)}, u32[]{:S(2)}) %all-to-all-start.21) | async-done | bytes 262176 | tf_op jit(solution)/shard_map/all_to_all | solution.py:17
  339.0 8.3 %all-to-all-done.22 = f32[16,32,128]{2,1,0:T(8,128)S(1)} async-done(((f32[16,32,128]{2,1,0:T(8,128)}), f32[16,32,128]{2,1,0:T(8,128)S(1)}, u32[]{:S(2)}, u32[]{:S(2)}) %all-to-all-start.22) | async-done | bytes 262176 | tf_op jit(solution)/shard_map/all_to_all | solution.py:17
  366.1 11.5 %all-to-all-done.2 = bf16[16,256,128]{2,1,0:T(8,128)(2,1)S(1)} async-done(((bf16[16,256,128]{2,1,0:T(8,128)(2,1)}), bf16[16,256,128]{2,1,0:T(8,128)(2,1)S(1)}, u32[]{:S(2)}, u32[]{:S(2)}) %all-to-all-start.2) | async-done | bytes 1048608 | tf_op jit(solution)/shard_map/all_to_all | solution.py:46
  384.8 9.8 %all-to-all-done.5 = bf16[16,256,128]{2,1,0:T(8,128)(2,1)S(1)} async-done(((bf16[16,256,128]{2,1,0:T(8,128)(2,1)}), bf16[16,256,128]{2,1,0:T(8,128)(2,1)S(1)}, u32[]{:S(2)}, u32[]{:S(2)}) %all-to-all-start.5) | async-done | bytes 1048608 | tf_op jit(solution)/shard_map/all_to_all | solution.py:46
  412.7 7.2 %all-to-all-start.11 = ((bf16[16,256,128]{2,1,0:T(8,128)(2,1)}), bf16[16,256,128]{2,1,0:T(8,128)(2,1)}, u32[]{:S(2)}, u32[]{:S(2)}) async-start(bf16[16,256,128]{2,1,0:T(8,128)(2,1)} %bitcast.50), calls=%async_computation.11 | async-start | bytes 2097152 | tf_op jit(solution)/shard_map/all_to_all | solution.py:46
  424.3 14.9 %all-to-all-done.11 = bf16[16,256,128]{2,1,0:T(8,128)(2,1)} async-done(((bf16[16,256,128]{2,1,0:T(8,128)(2,1)}), bf16[16,256,128]{2,1,0:T(8,128)(2,1)}, u32[]{:S(2)}, u32[]{:S(2)}) %all-to-all-start.11) | async-done | bytes 1048608 | tf_op jit(solution)/shard_map/all_to_all | solution.py:46
  446.1 15.0 %all-to-all-done.14 = bf16[16,256,128]{2,1,0:T(8,128)(2,1)S(1)} async-done(((bf16[16,256,128]{2,1,0:T(8,128)(2,1)}), bf16[16,256,128]{2,1,0:T(8,128)(2,1)S(1)}, u32[]{:S(2)}, u32[]{:S(2)}) %all-to-all-start.14) | async-done | bytes 1048608 | tf_op jit(solution)/shard_map/all_to_all | solution.py:46
  468.6 9.0 %all-to-all-done.17 = bf16[16,256,128]{2,1,0:T(8,128)(2,1)S(1)} async-done(((bf16[16,256,128]{2,1,0:T(8,128)(2,1)}), bf16[16,256,128]{2,1,0:T(8,128)(2,1)S(1)}, u32[]{:S(2)}, u32[]{:S(2)}) %all-to-all-start.17) | async-done | bytes 1048608 | tf_op jit(solution)/shard_map/all_to_all | solution.py:46
  (246 shorter events, 184.7 us)
Async XLA Ops:
  7.2 110.4 %all-gather.13.cloned.1.call-start = ((), (), s32[]{:S(2)}) async-start(), calls=%async_computation.24 | async-start | bytes 1114112 | tf_op jit(solution)/shard_map/all_gather | solution.py:55
  10.2 24.8 %all-to-all-start = ((bf16[16,256,128]{2,1,0:T(8,128)(2,1)}), bf16[16,256,128]{2,1,0:T(8,128)(2,1)S(1)}, u32[]{:S(2)}, u32[]{:S(2)}) async-start(bf16[16,256,128]{2,1,0:T(8,128)(2,1)} %broadcast_in_dim.36), calls=%async_computation | async-start | bytes 2097152 | tf_op jit(solution)/shard_map/all_to_all | solution.py:17
  17.3 124.2 %all-gather.23.cloned.1.call-start = ((), (), s32[]{:S(2)}) async-start(), calls=%async_computation.29 | async-start | bytes 1114112 | tf_op jit(solution)/shard_map/all_gather | solution.py:55
  55.2 18.4 %all-to-all-start.3 = ((bf16[16,256,128]{2,1,0:T(8,128)(2,1)}), bf16[16,256,128]{2,1,0:T(8,128)(2,1)S(1)}, u32[]{:S(2)}, u32[]{:S(2)}) async-start(bf16[16,256,128]{2,1,0:T(8,128)(2,1)} %broadcast_in_dim.38), calls=%async_computation.3 | async-start | bytes 2097152 | tf_op jit(solution)/shard_map/all_to_all | solution.py:17
  58.9 106.4 %all-gather.15.cloned.1.call-start = ((), (), s32[]{:S(2)}) async-start(), calls=%async_computation.25 | async-start | bytes 1114112 | tf_op jit(solution)/shard_map/all_gather | solution.py:55
  94.0 18.6 %all-to-all-start.6 = ((bf16[16,256,128]{2,1,0:T(8,128)(2,1)}), bf16[16,256,128]{2,1,0:T(8,128)(2,1)S(1)}, u32[]{:S(2)}, u32[]{:S(2)}) async-start(bf16[16,256,128]{2,1,0:T(8,128)(2,1)} %broadcast_in_dim.40), calls=%async_computation.6 | async-start | bytes 2097152 | tf_op jit(solution)/shard_map/all_to_all | solution.py:17
  97.7 90.7 %all-gather.21.cloned.1.call-start = ((), (), s32[]{:S(2)}) async-start(), calls=%async_computation.28 | async-start | bytes 1114112 | tf_op jit(solution)/shard_map/all_gather | solution.py:55
  113.9 19.1 %all-to-all-start.9 = ((bf16[16,256,128]{2,1,0:T(8,128)(2,1)}), bf16[16,256,128]{2,1,0:T(8,128)(2,1)S(1)}, u32[]{:S(2)}, u32[]{:S(2)}) async-start(bf16[16,256,128]{2,1,0:T(8,128)(2,1)} %broadcast_in_dim.42), calls=%async_computation.9 | async-start | bytes 2097152 | tf_op jit(solution)/shard_map/all_to_all | solution.py:17
  134.1 23.7 %all-to-all-start.1 = ((f32[16,1,8448]{2,1,0:T(1,128)}), f32[16,1,8448]{2,1,0:T(1,128)}, u32[]{:S(2)}, u32[]{:S(2)}) async-start(f32[16,1,8448]{2,1,0:T(1,128)} %broadcast_in_dim.37), calls=%async_computation.1 | async-start | bytes 1081344 | tf_op jit(solution)/shard_map/all_to_all | solution.py:17
  140.9 71.2 %all-gather.17.cloned.1.call-start = ((), (), s32[]{:S(2)}) async-start(), calls=%async_computation.26 | async-start | bytes 1114112 | tf_op jit(solution)/shard_map/all_gather | solution.py:55
  158.9 20.6 %all-to-all-start.16 = ((f32[16,1,8448]{2,1,0:T(1,128)}), f32[16,1,8448]{2,1,0:T(1,128)}, u32[]{:S(2)}, u32[]{:S(2)}) async-start(f32[16,1,8448]{2,1,0:T(1,128)} %broadcast_in_dim.47), calls=%async_computation.16 | async-start | bytes 1081344 | tf_op jit(solution)/shard_map/all_to_all | solution.py:17
  181.4 23.2 %all-to-all-start.4 = ((f32[16,1,8448]{2,1,0:T(1,128)}), f32[16,1,8448]{2,1,0:T(1,128)}, u32[]{:S(2)}, u32[]{:S(2)}) async-start(f32[16,1,8448]{2,1,0:T(1,128)} %broadcast_in_dim.39), calls=%async_computation.4 | async-start | bytes 1081344 | tf_op jit(solution)/shard_map/all_to_all | solution.py:17
  187.8 65.4 %all-gather.19.cloned.1.call-start = ((), (), s32[]{:S(2)}) async-start(), calls=%async_computation.27 | async-start | bytes 1114112 | tf_op jit(solution)/shard_map/all_gather | solution.py:55
  205.7 20.6 %all-to-all-start.13 = ((f32[16,1,8448]{2,1,0:T(1,128)}), f32[16,1,8448]{2,1,0:T(1,128)S(1)}, u32[]{:S(2)}, u32[]{:S(2)}) async-start(f32[16,1,8448]{2,1,0:T(1,128)} %broadcast_in_dim.45), calls=%async_computation.13 | async-start | bytes 1081344 | tf_op jit(solution)/shard_map/all_to_all | solution.py:17
  227.4 28.8 %all-to-all-start.7 = ((f32[16,1,8448]{2,1,0:T(1,128)}), f32[16,1,8448]{2,1,0:T(1,128)S(1)}, u32[]{:S(2)}, u32[]{:S(2)}) async-start(f32[16,1,8448]{2,1,0:T(1,128)} %broadcast_in_dim.41), calls=%async_computation.7 | async-start | bytes 1081344 | tf_op jit(solution)/shard_map/all_to_all | solution.py:17
  257.4 21.7 %all-to-all-start.10 = ((f32[16,1,8448]{2,1,0:T(1,128)}), f32[16,1,8448]{2,1,0:T(1,128)S(1)}, u32[]{:S(2)}, u32[]{:S(2)}) async-start(f32[16,1,8448]{2,1,0:T(1,128)} %broadcast_in_dim.43), calls=%async_computation.10 | async-start | bytes 1081344 | tf_op jit(solution)/shard_map/all_to_all | solution.py:17
  279.8 15.8 %all-to-all-start.18 = ((f32[16,32,128]{2,1,0:T(8,128)}), f32[16,32,128]{2,1,0:T(8,128)S(1)}, u32[]{:S(2)}, u32[]{:S(2)}) async-start(f32[16,32,128]{2,1,0:T(8,128)} %broadcast_in_dim.96), calls=%async_computation.18 | async-start | bytes 524288 | tf_op jit(solution)/shard_map/all_to_all | solution.py:17
  348.1 12.2 %all-to-all-start.23 = ((f32[16,32,128]{2,1,0:T(8,128)}), f32[16,32,128]{2,1,0:T(8,128)S(1)}, u32[]{:S(2)}, u32[]{:S(2)}) async-start(f32[16,32,128]{2,1,0:T(8,128)} %broadcast_in_dim.101), calls=%async_computation.23 | async-start | bytes 524288 | tf_op jit(solution)/shard_map/all_to_all | solution.py:17
  361.0 16.6 %all-to-all-start.2 = ((bf16[16,256,128]{2,1,0:T(8,128)(2,1)}), bf16[16,256,128]{2,1,0:T(8,128)(2,1)S(1)}, u32[]{:S(2)}, u32[]{:S(2)}) async-start(bf16[16,256,128]{2,1,0:T(8,128)(2,1)} %bitcast.11), calls=%async_computation.2 | async-start | bytes 2097152 | tf_op jit(solution)/shard_map/all_to_all | solution.py:46
  377.6 17.0 %all-to-all-start.5 = ((bf16[16,256,128]{2,1,0:T(8,128)(2,1)}), bf16[16,256,128]{2,1,0:T(8,128)(2,1)S(1)}, u32[]{:S(2)}, u32[]{:S(2)}) async-start(bf16[16,256,128]{2,1,0:T(8,128)(2,1)} %bitcast.24), calls=%async_computation.5 | async-start | bytes 2097152 | tf_op jit(solution)/shard_map/all_to_all | solution.py:46
  394.6 18.0 %all-to-all-start.8 = ((bf16[16,256,128]{2,1,0:T(8,128)(2,1)}), bf16[16,256,128]{2,1,0:T(8,128)(2,1)}, u32[]{:S(2)}, u32[]{:S(2)}) async-start(bf16[16,256,128]{2,1,0:T(8,128)(2,1)} %bitcast.37), calls=%async_computation.8 | async-start | bytes 2097152 | tf_op jit(solution)/shard_map/all_to_all | solution.py:46
  412.7 26.4 %all-to-all-start.11 = ((bf16[16,256,128]{2,1,0:T(8,128)(2,1)}), bf16[16,256,128]{2,1,0:T(8,128)(2,1)}, u32[]{:S(2)}, u32[]{:S(2)}) async-start(bf16[16,256,128]{2,1,0:T(8,128)(2,1)} %bitcast.50), calls=%async_computation.11 | async-start | bytes 2097152 | tf_op jit(solution)/shard_map/all_to_all | solution.py:46
  439.1 22.0 %all-to-all-start.14 = ((bf16[16,256,128]{2,1,0:T(8,128)(2,1)}), bf16[16,256,128]{2,1,0:T(8,128)(2,1)S(1)}, u32[]{:S(2)}, u32[]{:S(2)}) async-start(bf16[16,256,128]{2,1,0:T(8,128)(2,1)} %bitcast.63), calls=%async_computation.14 | async-start | bytes 2097152 | tf_op jit(solution)/shard_map/all_to_all | solution.py:46
  461.1 16.5 %all-to-all-start.17 = ((bf16[16,256,128]{2,1,0:T(8,128)(2,1)}), bf16[16,256,128]{2,1,0:T(8,128)(2,1)S(1)}, u32[]{:S(2)}, u32[]{:S(2)}) async-start(bf16[16,256,128]{2,1,0:T(8,128)(2,1)} %bitcast.76), calls=%async_computation.17 | async-start | bytes 2097152 | tf_op jit(solution)/shard_map/all_to_all | solution.py:46
  (56 other events, 994.9 us)
Sparse Core Ops, SparseCore 0:
  9.8 37.5 all-gather.12
  49.8 37.1 all-gather.22
  88.8 37.1 all-gather.14
  127.7 39.1 all-gather.20
  169.1 40.9 all-gather.16
  212.3 40.8 all-gather.18
where the time goes:
time: 489 us; the launch traced here: 485 us
  waiting for transfers between devices  248 us (51%)
  starting transfers between devices  110 us (22%)
  blocking collectives  37.8 us (8%)
  matrix products  28.8 us (6%)
  local copies, waits for them, and re-layouts  22.9 us (5%)
  other arithmetic  22.6 us (5%)
  between operations  15 us (3%)
    all_to_all x16, waiting for transfers between devices, from_everyone(): return lax.all_to_all(copies, axis, split_axis=0, concat_axis=0, tiled=True)  161 us
    all_to_all x16, starting transfers between devices, from_everyone(): return lax.all_to_all(copies, axis, split_axis=0, concat_axis=0, tiled=True)  83.2 us
    all_to_all x6, waiting for transfers between devices, sum_at_owner(): lax.all_to_all(pieces, axis, split_axis=0, concat_axis=0, tiled=True)  65.3 us
    all_to_all x2, blocking collectives, from_everyone(): return lax.all_to_all(copies, axis, split_axis=0, concat_axis=0, tiled=True)  37.8 us
    all_to_all x6, starting transfers between devices, sum_at_owner(): lax.all_to_all(pieces, axis, split_axis=0, concat_axis=0, tiled=True)  26.6 us
    all_gather x6, waiting for transfers between devices, one_layer(): grads_all = lax.all_gather(grads, 'row', axis=0, tiled=True)  19.5 us
    broadcast_in_dim x18, local copies, waits for them, and re-layouts, from_everyone(): copies = jnp.broadcast_to(shard, (lax.axis_size(axis), *shard.shape))  17.4 us
    dot_general x6, matrix products, one_layer(): lax.dot_general(gathered_copies(acts, 'col', 0), grads_all, (((0,), (0,))...  11.2 us
  transfers between devices with their start and end apart: 28, of which 22 were waited for; matrix products, arithmetic and copies ran while one was open for 13% of the time, Pallas kernels for 0%

commit v1 on v0

v1 whole, which is shorter than its diff:
```python
import functools

import jax
import jax.numpy as jnp
from jax import lax
from jax.experimental import pallas as pl
from jax.experimental.pallas import tpu as pltpu
from jax.sharding import PartitionSpec as P

F32 = jnp.float32
BF16 = jnp.bfloat16
HIGH = lax.Precision.HIGHEST
N = 16
ZS = 8
L = 6
NG = 3
GL = L // NG
CH = 512
NCH = 2048 // CH


def nn(a, b):
    return lax.dot_general(a, b, (((1,), (0,)), ((), ())), preferred_element_type=F32)


def nt(a, b):
    return lax.dot_general(a, b, (((1,), (1,)), ((), ())), preferred_element_type=F32)


def tn(a, b):
    return lax.dot_general(a, b, (((0,), (0,)), ((), ())), preferred_element_type=F32)


def exact(a, b):
    return lax.dot_general(a, b, (((1,), (0,)), ((), ())), precision=HIGH, preferred_element_type=F32)


def aligned(i, n):
    return pl.multiple_of(i * n, n)


def kernel(
    acts, grads, ain, mag, frozen, aout,
    o_in, o_ain, o_aout, o_mag,
    H, G, WA, MF, WM, SQ, SC, CR, PPb, PPr, PSb, PD, USb, USr, DL, D1r, D2r, OGr, IPf, IRr, IAr,
    in_s, t1s, t1r, t2s, t2r, rs, rr, ls, lr, ds, dr, ws, wr,
    sqs, sqr, scs, scr, p1s, p1r, p2s, p2r, pbs, pbr, uss, usr,
    d1s, d1r, d2s, d2r, d3s, d3r, ogs, ogr, irs, irr, ias, iar,
):
    r = lax.axis_index("row")
    c = lax.axis_index("col")
    z, k = r // 2, r % 2
    x, y = c // 4, c % 4

    def rcopy(src, dst, ss, rsem, **ids):
        return pltpu.make_async_remote_copy(
            src_ref=src, dst_ref=dst, send_sem=ss, recv_sem=rsem,
            device_id=ids, device_id_type=pl.DeviceIdType.MESH,
        )

    def landed(ref, sem):
        pltpu.make_async_copy(ref, ref, sem).wait()

    def to_row(make):
        def step(i, _):
            make(lax.rem(r + i, N)).start()
            return 0
        lax.fori_loop(1, N, step, 0)

    def to_col(make):
        def step(i, _):
            make(lax.rem(c + i, N)).start()
            return 0
        lax.fori_loop(1, N, step, 0)

    own = pl.ds(aligned(c, 128), 128)
    cf = pltpu.make_async_copy(frozen, WA.at[:, 0:128, own], in_s.at[0])
    ca = pltpu.make_async_copy(aout, WA.at[:, 128:160, own], in_s.at[1])
    cf.start()
    ca.start()

    barrier = pltpu.get_barrier_semaphore()

    def greet(i, _):
        pl.semaphore_signal(barrier, inc=1, device_id={"row": lax.rem(r + i, N)}, device_id_type=pl.DeviceIdType.MESH)
        pl.semaphore_signal(barrier, inc=1, device_id={"col": lax.rem(c + i, N)}, device_id_type=pl.DeviceIdType.MESH)
        return 0

    lax.fori_loop(1, N, greet, 0)
    pl.semaphore_wait(barrier, 2 * (N - 1))

    def layers(g):
        return pl.ds(GL * g, GL)

    for g in range(NG):
        to_row(lambda p, g=g: rcopy(
            grads.at[layers(g), pl.ds(aligned(p, 16), 16), :], H.at[r, layers(g)],
            t1s.at[g], t1r.at[g], row=p))
    H[r] = grads[:, pl.ds(aligned(r, 16), 16), :]

    cf.wait()
    ca.wait()

    def place_of(h, a, b):
        return 4 * b + a if h == 0 else 4 * a + b

    pos = ((y, x), (x, y))

    def wblock(h, a, b, lo=0, hi=160):
        return WA.at[pl.ds(3 * h, 3), lo:hi, pl.ds(aligned(place_of(h, a, b), 128), 128)]

    def mod4(i):
        return lax.rem(i + 4, 4)

    def w_copy(h, kind, slot, a, b, target):
        lo, hi = ((0, 160), (0, 160), (0, 80), (80, 160))[kind]
        ref = wblock(h, a, b, lo, hi)
        return rcopy(ref, ref, ws.at[h, slot, kind], wr.at[h, slot, kind], col=target)

    def first(h, kind, j):
        a, b = pos[h]
        step = 1 if kind in (0, 2) else -1
        return w_copy(h, kind, 0, mod4(a + j), b, place_of(h, mod4(a + step), b))

    def second(h, kind, slot, j, jb):
        a, b = pos[h]
        step = 1 if kind in (0, 2) else -1
        return w_copy(h, kind, slot, mod4(a + j), mod4(b + jb), place_of(h, a, mod4(b + step)))

    def first_landed(h, kind):
        a, b = pos[h]
        j = (-1, 1, 2, 2)[kind]
        lo, hi = ((0, 160), (0, 160), (0, 80), (80, 160))[kind]
        landed(wblock(h, mod4(a + j), b, lo, hi), wr.at[h, 0, kind])

    def second_landed(h, kind, slot, j):
        a, b = pos[h]
        jb = (-1, 1, 2, 2)[kind]
        lo, hi = ((0, 160), (0, 160), (0, 80), (80, 160))[kind]
        landed(wblock(h, mod4(a + j), mod4(b + jb), lo, hi), wr.at[h, slot, kind])

    offsets = ((1, 0), (2, -1), (3, 1), (4, 2))

    def second_out(h, slot, j):
        second(h, 0, slot, j, 0).start()
        second(h, 1, slot, j, 0).start()

    def second_on(h, slot, j):
        second_landed(h, 0, slot, j)
        second(h, 2, slot, j, -1).start()
        second_landed(h, 1, slot, j)
        second(h, 3, slot, j, 1).start()

    for h in range(2):
        first(h, 0, 0).start()
        first(h, 1, 0).start()
    for h in range(2):
        second_out(h, 1, 0)

    rows = lax.broadcasted_iota(jnp.int32, (256, 32), 0)
    ranks = lax.broadcasted_iota(jnp.int32, (256, 32), 1)

    def spread(i):
        off = rows % 16 - 2 * i
        return jnp.where((off >= 0) & (off < 2) & (ranks == rows // 16 * 2 + off), 1.0, 0.0).astype(F32)

    back_rows = lax.broadcasted_iota(jnp.int32, (32, 256), 1)
    back_ranks = lax.broadcasted_iota(jnp.int32, (32, 256), 0)

    def collect(i):
        off = back_rows % 16 - 2 * i
        return jnp.where((off >= 0) & (off < 2) & (back_ranks == back_rows // 16 * 2 + off), 1.0, 0.0).astype(F32)

    SQ[...] = jnp.zeros((8, 128), F32)
    part = jnp.zeros((256, 256), F32)
    inner = jnp.zeros((256, 128), F32)
    for i in range(L):
        block = WA[i, 0:128, own].astype(F32) + tn(ain[i], WA[i, 128:160, own])
        SQ[i : i + 1] = jnp.sum(block * block, axis=0, keepdims=True)
        wide = nn(spread(i).astype(BF16), ain[i]).astype(BF16)
        part += nt(wide, acts[i])
        high = block.astype(BF16)
        inner += nn(wide, high) + nn(wide, (block - high.astype(F32)).astype(BF16))
    PPb[...] = part.astype(BF16).reshape(N, 16, 256)
    USb[:, 16:32, :] = inner.astype(BF16).reshape(N, 16, 128)
    SQr = SQ_all = D2r.at[1]
    SQr[r] = SQ[...]
    to_row(lambda p: rcopy(SQ, SQ_all.at[r], sqs, sqr, row=p))
    PPr[r] = PPb[r]
    to_row(lambda p: rcopy(PPb.at[p], PPr.at[r], p1s, p1r, row=p))

    for g in range(NG):
        landed(H.at[0 : N - 1, layers(g)], t1r.at[g])
        mine = pl.ds(aligned(r, 16), 16)
        to_col(lambda q, g=g: rcopy(
            H.at[q, layers(g)], G.at[layers(g), pl.ds(aligned(r, 16), 16), pl.ds(aligned(c, 128), 128)],
            t2s.at[g], t2r.at[g], col=q))
        G[GL * g : GL * g + GL, mine, own] = H[c, GL * g : GL * g + GL]

    for h in range(2):
        first_landed(h, 0)
        first(h, 2, -1).start()
        second_out(h, 2, -1)
        first_landed(h, 1)
        first(h, 3, 1).start()
        second_out(h, 3, 1)

    landed(SQ_all.at[0 : N - 1], sqr)
    squares = SQr[0]
    for p in range(1, N):
        squares = squares + SQr[p]
    norms = jnp.sqrt(squares[0:L] + 0.25)
    scales = mag[...] / norms

    landed(PPr.at[0 : N - 1], p1r)
    total = PPr[0].astype(F32)
    for p in range(1, N):
        total = total + PPr[p].astype(F32)
    PSb[...] = total.astype(BF16)

    def chunk(g, q, count=GL, at=0):
        return G.at[pl.ds(GL * g + at, count), pl.ds(aligned(q, 16), 16), :]

    def across(i):
        return lax.rem(z + i + ZS, ZS) * 2 + k

    def right(g, s):
        ref = chunk(g, across(-s)) if s < 3 else chunk(g, across(-s), 1, 0)
        return rcopy(ref, ref, rs.at[g, s], rr.at[g, s], row=across(1))

    def left(g, s):
        ref = chunk(g, across(s)) if s < 3 else chunk(g, across(s), 1, 1)
        return rcopy(ref, ref, ls.at[g, s], lr.at[g, s], row=across(-1))

    partner = z * 2 + 1 - k

    def over(g, n, i):
        ref = chunk(g, across(i))
        return rcopy(ref, ref, ds.at[g, n], dr.at[g, n], row=partner)

    hops = (0, -1, -2, -3, 1, 2, 3, 4)

    def ring(g, s):
        if s == 0:
            landed(G.at[layers(g), pl.ds(aligned(r, 16), 16), 0 : 128 * (N - 1)], t2r.at[g])
            right(g, 0).start()
            left(g, 0).start()
            over(g, 0, 0).start()
        elif s < 4:
            landed(chunk(g, across(-s)), rr.at[g, s - 1])
            right(g, s).start()
            landed(chunk(g, across(s)), lr.at[g, s - 1])
            left(g, s).start()
            over(g, s, -s).start()
            over(g, 3 + s, s).start()
        else:
            landed(chunk(g, across(4), 1, 0), rr.at[g, 3])
            landed(chunk(g, across(4), 1, 1), lr.at[g, 3])
            over(g, 7, 4).start()

    def ring_landed(g):
        for n, i in enumerate(hops):
            landed(chunk(g, lax.rem(z + i + ZS, ZS) * 2 + 1 - k), dr.at[g, n])

    ring(0, 0)

    for i in range(L):
        SC[i : i + 1, own] = scales[i : i + 1]
    SCs = SQ
    landed(SQr.at[0 : N - 1], sqs)
    SCs[0:L] = scales
    to_col(lambda q: rcopy(SCs, SC.at[:, own], scs, scr, col=q))

    @pl.when(c != r)
    def _():
        rcopy(PSb, PD.at[r], p2s, p2r, row=c).start()

    @pl.when(c == r)
    def _():
        PD[r] = PSb[...]

    ring(1, 0)
    ring(0, 1)
    ring(2, 0)

    for h in range(2):
        second_on(h, 1, 0)
    for h in range(2):
        first_landed(h, 2)
        first_landed(h, 3)
        second_out(h, 4, 2)

    ring(1, 1)
    ring(0, 2)

    @pl.when(c == r)
    def _():
        landed(PD.at[0 : N - 1], p2r)
        to_col(lambda q: rcopy(PD, PD, pbs.at[lax.rem(q - c + N, N)], pbr, col=q))

    for h in range(2):
        second_on(h, 2, -1)
        second_on(h, 3, 1)

    ring(2, 1)
    ring(1, 2)
    ring(0, 3)

    @pl.when(c != r)
    def _():
        landed(PD, pbr)

    kind = lax.broadcasted_iota(jnp.int32, (256, 128), 0) % 16 // 2
    low = PD[...].reshape(N * 16, 256)
    inner_outer = jnp.zeros((256, 128), F32)
    for i in range(L):
        inner_outer = jnp.where(kind == i, nn(low, grads[i]), inner_outer)
    USb[:, 0:16, :] = inner_outer.astype(BF16).reshape(N, 16, 128)
    USr[r] = USb[r]
    to_row(lambda p: rcopy(USb.at[p], USr.at[r], uss, usr, row=p))

    for h in range(2):
        second_on(h, 4, 2)

    ring(2, 2)
    ring(1, 3)
    ring(0, 4)

    for h in range(2):
        for slot, j in offsets:
            second_landed(h, 2, slot, j)
            second_landed(h, 3, slot, j)

    landed(D1r.at[0 : N - 1], scr)

    def prepare(i):
        for n in range(NCH):
            cols = pl.ds(n * CH, CH)
            merged = WA[i, 0:128, cols].astype(F32) + tn(ain[i], WA[i, 128:160, cols])
            MF[i, :, cols] = merged
            WM[i, :, cols] = merged.astype(BF16)

    DL[...] = jnp.zeros((8, 2048), F32)

    def dots_of(i):
        for n in range(NCH):
            cols = pl.ds(n * CH, CH)
            outer = tn(acts[i], G[i, :, cols])
            DL[i : i + 1, cols] = jnp.sum(MF[i, :, cols] * outer, axis=0, keepdims=True)

    def grads_of(i):
        got = jnp.zeros((256, 128), F32)
        low_t = jnp.zeros((32, 256), F32)
        for n in range(NCH):
            cols = pl.ds(n * CH, CH)
            scaled = (G[i, :, cols].astype(F32) * SC[i : i + 1, cols]).astype(BF16)
            got += nt(scaled, WM[i, :, cols])
            low_t += nt(WA[i, 128:160, cols], scaled)
        o_in[i] = got.astype(BF16)
        high = low_t.astype(BF16)
        rest = (low_t - high.astype(F32)).astype(BF16)
        return nn(high, acts[i]) + nn(rest, acts[i])

    for i in range(L):
        prepare(i)
    ring(2, 3)
    ring(1, 4)

    in_part = jnp.zeros((256, 128), F32)

    def placed(i, x):
        return exact(spread(i), x)

    for i in range(0, GL):
        if i == 0:
            ring_landed(0)
        dots_of(i)
        in_part += placed(i, grads_of(i))
    ring(2, 4)
    ring_landed(1)
    for i in range(GL, 2 * GL):
        dots_of(i)
        in_part += placed(i, grads_of(i))
    ring_landed(2)
    for i in range(2 * GL, L):
        dots_of(i)

    D1r[c] = DL[:, own]
    to_col(lambda q: rcopy(DL.at[:, pl.ds(aligned(q, 128), 128)], D1r.at[c], d1s, d1r, col=q))
    for i in range(2 * GL, L):
        in_part += placed(i, grads_of(i))
    IPf[...] = in_part.reshape(N, 16, 128)
    IRr[c] = IPf[c]
    to_col(lambda q: rcopy(IPf.at[q], IRr.at[c], irs, irr, col=q))

    landed(D1r.at[0 : N - 1], d1r)
    sub = D1r[0]
    for p in range(1, N):
        sub = sub + D1r[p]
    landed(SQr.at[0 : N - 1], scs)
    SQ[...] = sub
    D2 = D2r.at[0]
    D2[r] = sub
    to_row(lambda p: rcopy(SQ, D2.at[r], d2s, d2r, row=p))

    landed(USr.at[0 : N - 1], usr)
    both = USr[0].astype(F32)
    for p in range(1, N):
        both = both + USr[p].astype(F32)

    landed(IRr.at[0 : N - 1], irr)
    in_sum = IRr[0]
    for p in range(1, N):
        in_sum = in_sum + IRr[p]
    IAr[c] = in_sum
    to_col(lambda q: rcopy(IAr.at[c], IAr.at[c], ias, iar, col=q))

    landed(D2.at[0 : N - 1], d2r)
    dots8 = D2[0]
    for p in range(1, N):
        dots8 = dots8 + D2[p]
    dots = dots8[0:L]
    o_mag[...] = dots / norms
    correct = -mag[...] * dots / (norms * norms * norms)
    for i in range(L):
        CR[i : i + 1, own] = correct[i : i + 1]
    landed(D1r.at[0 : N - 1], d1s)
    landed(D2.at[0 : N - 1], d2s)
    SQ[0:L] = correct
    to_col(lambda q: rcopy(SQ, CR.at[:, own], d3s, d3r, col=q))
    out = jnp.zeros((16, 128), F32)
    kind16 = lax.broadcasted_iota(jnp.int32, (16, 128), 0) // 2
    for i in range(L):
        out = jnp.where(kind16 == i, both[0:16] * scales[i : i + 1] + both[16:32] * correct[i : i + 1], out)
    OGr[r] = out
    to_row(lambda p: rcopy(OGr.at[r], OGr.at[r], ogs, ogr, row=p))

    landed(D1r.at[0 : N - 1], d3r)
    landed(IAr.at[0 : N - 1], iar)
    in_all = IAr[...].reshape(N * 16, 128)
    for i in range(L):
        second_term = jnp.zeros((32, 128), F32)
        for n in range(NCH):
            cols = pl.ds(n * CH, CH)
            scaled_out = WA[i, 128:160, cols].astype(F32) * CR[i : i + 1, cols]
            high = scaled_out.astype(BF16)
            rest = (scaled_out - high.astype(F32)).astype(BF16)
            second_term += nt(high, WM[i, :, cols]) + nt(rest, WM[i, :, cols])
        o_ain[i] = exact(collect(i), in_all) + second_term

    landed(OGr.at[0 : N - 1], ogr)
    out_all = OGr[...].reshape(N * 16, 128)
    for i in range(L):
        o_aout[i] = exact(collect(i), out_all)

    for g in range(NG):
        landed(H.at[0 : N - 1, layers(g)], t1s.at[g])
        landed(H.at[0 : N - 1, layers(g)], t2s.at[g])
        for s in range(4):
            right(g, s).wait_send()
            left(g, s).wait_send()
        for n, i in enumerate(hops):
            over(g, n, i).wait_send()
    for h in range(2):
        for n, j in enumerate((0, 0, -1, 1)):
            first(h, n, j).wait_send()
        for slot, j in offsets:
            for n, jb in enumerate((0, 0, -1, 1)):
                second(h, n, slot, j, jb).wait_send()
    landed(PPr.at[0 : N - 1], p1s)
    landed(USr.at[0 : N - 1], uss)
    landed(D1r.at[0 : N - 1], d3s)
    landed(OGr.at[0 : N - 1], ogs)
    landed(IRr.at[0 : N - 1], irs)
    landed(IAr.at[0 : N - 1], ias)

    @pl.when(c != r)
    def _():
        landed(PSb, p2s)

    @pl.when(c == r)
    def _():
        def drain(i, _):
            landed(PD, pbs.at[i])
            return 0
        lax.fori_loop(1, N, drain, 0)


def body(attn_out, out_cotangent, frozen, adapt_in, adapt_out, magnitude):
    dma = pltpu.SemaphoreType.DMA
    vmem = pl.BlockSpec(memory_space=pltpu.VMEM)
    anywhere = pl.BlockSpec(memory_space=pl.ANY)
    V = pltpu.VMEM
    scratch = [
        V((N, L, 16, 128), BF16),
        V((L, 256, 2048), BF16),
        V((L, 160, 2048), BF16),
        V((L, 128, 2048), F32),
        V((L, 128, 2048), BF16),
        V((8, 128), F32),
        V((8, 2048), F32),
        V((8, 2048), F32),
        V((N, 16, 256), BF16),
        V((N, 16, 256), BF16),
        V((16, 256), BF16),
        V((N, 16, 256), BF16),
        V((N, 32, 128), BF16),
        V((N, 32, 128), BF16),
        V((8, 2048), F32),
        V((N, 8, 128), F32),
        V((2, N, 8, 128), F32),
        V((N, 16, 128), F32),
        V((N, 16, 128), F32),
        V((N, 16, 128), F32),
        V((N, 16, 128), F32),
        dma((2,)),
        dma((NG,)), dma((NG,)), dma((NG,)), dma((NG,)),
        dma((NG, 4)), dma((NG, 4)), dma((NG, 4)), dma((NG, 4)),
        dma((NG, 8)), dma((NG, 8)),
        dma((2, 5, 4)), dma((2, 5, 4)),
        dma, dma, dma, dma, dma, dma, dma, dma,
        dma((N,)), dma, dma, dma,
        dma, dma, dma, dma, dma, dma, dma, dma, dma, dma, dma, dma,
    ]
    return pl.pallas_call(
        kernel,
        out_shape=(
            jax.ShapeDtypeStruct((L, 256, 128), BF16),
            jax.ShapeDtypeStruct((L, 32, 128), F32),
            jax.ShapeDtypeStruct((L, 32, 128), F32),
            jax.ShapeDtypeStruct((L, 128), F32),
        ),
        in_specs=[vmem, vmem, vmem, vmem, anywhere, anywhere],
        out_specs=(vmem, vmem, vmem, vmem),
        scratch_shapes=scratch,
        compiler_params=pltpu.CompilerParams(
            collective_id=0, has_side_effects=True, vmem_limit_bytes=48 * 1024 * 1024
        ),
        name="dora",
    )(attn_out, out_cotangent, adapt_in, magnitude, frozen, adapt_out)


def solution(mesh):
    return jax.shard_map(
        body,
        mesh=mesh,
        in_specs=(
            P(None, "col", "row"),
            P(None, "row", "col"),
            P(None, "row", "col"),
            P(None, None, "row"),
            P(None, None, "col"),
            P(None, "col"),
        ),
        out_specs=(
            P(None, "col", "row"),
            P(None, None, "row"),
            P(None, None, "col"),
            P(None, "col"),
        ),
        check_vma=False,
    )
```

time: 489 us -> 97.1 us (0.20)
  the two profiles are of different devices: /device:TPU:160 before, /device:TPU:1 now
where the time goes in v1:
time: 97.1 us; the launch traced here: 96.8 us
  Pallas kernels  88.3 us (91%)
  local copies, waits for them, and re-layouts  7.81 us (8%)
    pallas_call x1, Pallas kernels, body(): pl.pallas_call(kernel, out_shape=(jax.ShapeDtypeStruct((L, 256, 128), BF1...  88.3 us
    unnamed x16, local copies, waits for them, and re-layouts  7.81 us

profile of v1, /device:TPU:1, one launch (start us, length us, event | category | flops | bytes accessed | tf_op | source)
XLA Modules:
  0.0 96.8 jit_solution(6440622565444885895)
XLA Ops:
  0.6 0.0 copy-start
  0.6 1.0 %copy-done = bf16[6,256,128]{2,1,0:T(8,128)(2,1)S(1)} copy-done((bf16[6,256,128]{2,1,0:T(8,128)(2,1)S(1)}, bf16[6,256,128]{2,1,0:T(8,128)(2,1)}, u32[]{:S(2)}) %copy-start) | copy-done | bytes 393240
  1.6 0.0 copy-start.1
  1.6 1.0 %copy-done.1 = bf16[6,256,128]{2,1,0:T(8,128)(2,1)S(1)} copy-done((bf16[6,256,128]{2,1,0:T(8,128)(2,1)S(1)}, bf16[6,256,128]{2,1,0:T(8,128)(2,1)}, u32[]{:S(2)}) %copy-start.1) | copy-done | bytes 393240
  2.6 0.0 copy-start.2
  2.6 0.9 copy-done.2
  3.6 0.0 copy-start.3
  3.6 0.8 copy-done.3
  4.4 0.0 copy-start.4
  4.4 0.8 copy-done.4
  5.2 0.0 copy-start.5
  5.2 0.7 copy-done.5
  5.8 88.3 %dora.1 = (bf16[6,256,128]{2,1,0:T(8,128)(2,1)S(1)}, f32[6,32,128]{2,1,0:T(8,128)S(1)}, f32[6,32,128]{2,1,0:T(8,128)S(1)}, f32[6,128]{1,0:T(8,128)S(1)}) custom-call(bf16[6,256,128]{2,1,0:T(8,128)(2,1)S(1)} %copy-done, bf16[6,256,128]{2,1,0:T(8,128)(2,1)S(1)} %copy-done.1, bf16[6,32,128]{2,1,0:T(8,128)(2,1)S(1)} %copy-done.3, f32[6,128]{1,0:T(8,128)S(1)} %copy-done.5, ...), custom_call_target="tpu_custom_call" | custom-call | tf_op jit(solution)/shard_map/dora/pallas_call | solution.py:525
  94.2 0.7 copy.14
  94.9 0.6 copy.15
  95.6 0.6 copy.16
  96.2 0.6 copy.17
Async XLA Ops:
  0.6 1.0 %copy-start = (bf16[6,256,128]{2,1,0:T(8,128)(2,1)S(1)}, bf16[6,256,128]{2,1,0:T(8,128)(2,1)}, u32[]{:S(2)}) copy-start(bf16[6,256,128]{2,1,0:T(8,128)(2,1)} %acts.1) | copy-start | bytes 1179652
  1.6 1.0 %copy-start.1 = (bf16[6,256,128]{2,1,0:T(8,128)(2,1)S(1)}, bf16[6,256,128]{2,1,0:T(8,128)(2,1)}, u32[]{:S(2)}) copy-start(bf16[6,256,128]{2,1,0:T(8,128)(2,1)} %grads.1) | copy-start | bytes 1179652
  2.6 0.9 copy-start.2
  3.6 0.8 copy-start.3
  4.4 0.8 copy-start.4
  5.2 0.7 copy-start.5

commit v2 on v0

v2 whole, which is shorter than its diff:
```python
import functools

import jax
import jax.numpy as jnp
from jax import lax
from jax.experimental import pallas as pl
from jax.experimental.pallas import tpu as pltpu
from jax.sharding import PartitionSpec as P

F32 = jnp.float32
BF16 = jnp.bfloat16
HIGH = lax.Precision.HIGHEST
N = 16
ZS = 8
L = 6
NG = 3
GL = L // NG
CH = 512
NCH = 2048 // CH


def nn(a, b):
    return lax.dot_general(a, b, (((1,), (0,)), ((), ())), preferred_element_type=F32)


def nt(a, b):
    return lax.dot_general(a, b, (((1,), (1,)), ((), ())), preferred_element_type=F32)


def tn(a, b):
    return lax.dot_general(a, b, (((0,), (0,)), ((), ())), preferred_element_type=F32)


def exact(a, b):
    return lax.dot_general(a, b, (((1,), (0,)), ((), ())), precision=HIGH, preferred_element_type=F32)


def aligned(i, n):
    return pl.multiple_of(i * n, n)


def kernel(
    h_acts, h_grads, h_ain, h_mag, h_frozen, h_aout,
    h_in, h_ain_grad, h_aout_grad, h_mag_grad,
    acts, grads, ain, mag, o_in, o_ain, o_aout, o_mag,
    H, G, WA, MF, WM, SQ, SQr, SC, CR, PPb, PPr, PSb, PD, PE, USb, USr, DL, D1r, D2r, OGr, IPf, IRr, IAr,
    in_s, out_s, t1s, t1r, t2s, t2r, rs, rr, ls, lr, ds, dr, ws, wr,
    sqs, sqr, scs, scr, p1s, p1r, p2s, p2r, pbs, pbr, uss, usr,
    d1s, d1r, d2s, d2r, d3s, d3r, ogs, ogr, irs, irr, ias, iar,
):
    r = lax.axis_index("row")
    c = lax.axis_index("col")
    z, k = r // 2, r % 2
    x, y = c // 4, c % 4
    scope = jax.named_scope

    def rcopy(src, dst, ss, rsem, **ids):
        return pltpu.make_async_remote_copy(
            src_ref=src, dst_ref=dst, send_sem=ss, recv_sem=rsem,
            device_id=ids, device_id_type=pl.DeviceIdType.MESH,
        )

    def landed(ref, sem):
        pltpu.make_async_copy(ref, ref, sem).wait()

    def to_row(make):
        def step(i, _):
            make(lax.rem(r + i, N)).start()
            return 0
        lax.fori_loop(1, N, step, 0)

    def to_col(make):
        def step(i, _):
            make(lax.rem(c + i, N)).start()
            return 0
        lax.fori_loop(1, N, step, 0)

    own = pl.ds(aligned(c, 128), 128)
    mine = pl.ds(aligned(r, 16), 16)

    def layers(g):
        return pl.ds(GL * g, GL)

    loads = [
        pltpu.make_async_copy(h_grads, grads, in_s.at[0]),
        pltpu.make_async_copy(h_frozen, WA.at[:, 0:128, own], in_s.at[1]),
        pltpu.make_async_copy(h_aout, WA.at[:, 128:160, own], in_s.at[2]),
        pltpu.make_async_copy(h_ain, ain, in_s.at[3]),
        pltpu.make_async_copy(h_acts, acts, in_s.at[4]),
        pltpu.make_async_copy(h_mag, mag, in_s.at[5]),
    ]
    with scope("s00_barrier"):
        barrier = pltpu.get_barrier_semaphore()

        def greet(i, _):
            pl.semaphore_signal(barrier, inc=1, device_id={"row": lax.rem(r + i, N)}, device_id_type=pl.DeviceIdType.MESH)
            pl.semaphore_signal(barrier, inc=1, device_id={"col": lax.rem(c + i, N)}, device_id_type=pl.DeviceIdType.MESH)
            return 0

        lax.fori_loop(1, N, greet, 0)
        for load in loads:
            load.start()
        for load in loads:
            load.wait()
        H[r] = grads[:, mine, :]
        pl.semaphore_wait(barrier, 2 * (N - 1))

    with scope("s01_t1send"):
        for g in range(NG):
            to_row(lambda p, g=g: rcopy(
                grads.at[layers(g), pl.ds(aligned(p, 16), 16), :], H.at[r, layers(g)],
                t1s.at[g], t1r.at[g], row=p))

    def place_of(h, a, b):
        return 4 * b + a if h == 0 else 4 * a + b

    pos = ((y, x), (x, y))
    cuts = ((0, 160), (0, 160), (0, 80), (80, 160))

    def wblock(h, a, b, lo=0, hi=160):
        return WA.at[pl.ds(3 * h, 3), lo:hi, pl.ds(aligned(place_of(h, a, b), 128), 128)]

    def mod4(i):
        return lax.rem(i + 4, 4)

    def w_copy(h, kind, slot, a, b, target):
        ref = wblock(h, a, b, *cuts[kind])
        return rcopy(ref, ref, ws.at[h, slot, kind], wr.at[h, slot, kind], col=target)

    def first(h, kind, j):
        a, b = pos[h]
        step = 1 if kind in (0, 2) else -1
        return w_copy(h, kind, 0, mod4(a + j), b, place_of(h, mod4(a + step), b))

    def second(h, kind, slot, j, jb):
        a, b = pos[h]
        step = 1 if kind in (0, 2) else -1
        return w_copy(h, kind, slot, mod4(a + j), mod4(b + jb), place_of(h, a, mod4(b + step)))

    def first_landed(h, kind):
        a, b = pos[h]
        landed(wblock(h, mod4(a + (-1, 1, 2, 2)[kind]), b, *cuts[kind]), wr.at[h, 0, kind])

    def second_landed(h, kind, slot, j):
        a, b = pos[h]
        landed(wblock(h, mod4(a + j), mod4(b + (-1, 1, 2, 2)[kind]), *cuts[kind]), wr.at[h, slot, kind])

    offsets = ((1, 0), (2, -1), (3, 1), (4, 2))

    def second_out(h, slot, j):
        second(h, 0, slot, j, 0).start()
        second(h, 1, slot, j, 0).start()

    def second_on(slot):
        with scope(f"w_on{slot}"):
            j = dict(offsets)[slot]
            for h in range(2):
                second_landed(h, 0, slot, j)
                second(h, 2, slot, j, -1).start()
                second_landed(h, 1, slot, j)
                second(h, 3, slot, j, 1).start()

    for h in range(2):
        first(h, 0, 0).start()
        first(h, 1, 0).start()
    for h in range(2):
        second_out(h, 1, 0)

    rows = lax.broadcasted_iota(jnp.int32, (256, 32), 0)
    ranks = lax.broadcasted_iota(jnp.int32, (256, 32), 1)

    def spread(i):
        off = rows % 16 - 2 * i
        return jnp.where((off >= 0) & (off < 2) & (ranks == rows // 16 * 2 + off), 1.0, 0.0).astype(F32)

    back_rows = lax.broadcasted_iota(jnp.int32, (32, 256), 1)
    back_ranks = lax.broadcasted_iota(jnp.int32, (32, 256), 0)

    def collect(i):
        off = back_rows % 16 - 2 * i
        return jnp.where((off >= 0) & (off < 2) & (back_ranks == back_rows // 16 * 2 + off), 1.0, 0.0).astype(F32)

    with scope("s02_local"):
        SQ[...] = jnp.zeros((8, 128), F32)
        part = jnp.zeros((256, 256), F32)
        inner = jnp.zeros((256, 128), F32)
        for i in range(L):
            block = WA[i, 0:128, own].astype(F32) + tn(ain[i], WA[i, 128:160, own])
            SQ[i : i + 1] = jnp.sum(block * block, axis=0, keepdims=True)
            wide = nn(spread(i).astype(BF16), ain[i]).astype(BF16)
            part += nt(wide, acts[i])
            high = block.astype(BF16)
            inner += nn(wide, high) + nn(wide, (block - high.astype(F32)).astype(BF16))
        PPb[...] = part.astype(BF16).reshape(N, 16, 256)
        USb[:, 16:32, :] = inner.astype(BF16).reshape(N, 16, 128)
        SQr[r] = SQ[...]
        to_row(lambda p: rcopy(SQ, SQr.at[r], sqs, sqr, row=p))
        PPr[r] = PPb[r]
        to_row(lambda p: rcopy(PPb.at[p], PPr.at[r], p1s, p1r, row=p))

    def exchange(g):
        with scope(f"t2_{g}"):
            landed(H.at[0 : N - 1, layers(g)], t1r.at[g])
            to_col(lambda q: rcopy(
                H.at[q, layers(g)], G.at[layers(g), mine, own], t2s.at[g], t2r.at[g], col=q))
            G[GL * g : GL * g + GL, mine, own] = H[c, GL * g : GL * g + GL]

    def chunk(g, q, count=GL, at=0):
        return G.at[pl.ds(GL * g + at, count), pl.ds(aligned(q, 16), 16), :]

    def across(i):
        return lax.rem(z + i + ZS, ZS) * 2 + k

    def right(g, s):
        ref = chunk(g, across(-s)) if s < 3 else chunk(g, across(-s), 1, 0)
        return rcopy(ref, ref, rs.at[g, s], rr.at[g, s], row=across(1))

    def left(g, s):
        ref = chunk(g, across(s)) if s < 3 else chunk(g, across(s), 1, 1)
        return rcopy(ref, ref, ls.at[g, s], lr.at[g, s], row=across(-1))

    partner = z * 2 + 1 - k

    def over(g, n, i):
        ref = chunk(g, across(i))
        return rcopy(ref, ref, ds.at[g, n], dr.at[g, n], row=partner)

    hops = (0, -1, -2, -3, 1, 2, 3, 4)

    def ring(g, s):
        with scope(f"r{g}{s}"):
            if s == 0:
                landed(G.at[layers(g), mine, 0 : 128 * (N - 1)], t2r.at[g])
                right(g, 0).start()
                left(g, 0).start()
                over(g, 0, 0).start()
            elif s < 4:
                landed(chunk(g, across(-s)), rr.at[g, s - 1])
                right(g, s).start()
                landed(chunk(g, across(s)), lr.at[g, s - 1])
                left(g, s).start()
                over(g, s, -s).start()
                over(g, 3 + s, s).start()
            else:
                landed(chunk(g, across(4), 1, 0), rr.at[g, 3])
                landed(chunk(g, across(4), 1, 1), lr.at[g, 3])
                over(g, 7, 4).start()

    def ring_landed(g):
        with scope(f"r{g}_landed"):
            for n, i in enumerate(hops):
                landed(chunk(g, lax.rem(z + i + ZS, ZS) * 2 + 1 - k), dr.at[g, n])

    def prepare(i):
        with scope(f"prep{i}"):
            for n in range(NCH):
                cols = pl.ds(n * CH, CH)
                merged = WA[i, 0:128, cols].astype(F32) + tn(ain[i], WA[i, 128:160, cols])
                MF[i, :, cols] = merged
                WM[i, :, cols] = merged.astype(BF16)

    def dots_of(i):
        with scope(f"dots{i}"):
            for n in range(NCH):
                cols = pl.ds(n * CH, CH)
                outer = tn(acts[i], G[i, :, cols])
                DL[i : i + 1, cols] = jnp.sum(MF[i, :, cols] * outer, axis=0, keepdims=True)

    def grads_of(i):
        with scope(f"grads{i}"):
            got = jnp.zeros((256, 128), F32)
            low_t = jnp.zeros((32, 256), F32)
            for n in range(NCH):
                cols = pl.ds(n * CH, CH)
                scaled = (G[i, :, cols].astype(F32) * SC[i : i + 1, cols]).astype(BF16)
                got += nt(scaled, WM[i, :, cols])
                low_t += nt(WA[i, 128:160, cols], scaled)
            o_in[i] = got.astype(BF16)
            high = low_t.astype(BF16)
            rest = (low_t - high.astype(F32)).astype(BF16)
            new = exact(spread(i), nn(high, acts[i]) + nn(rest, acts[i])).reshape(N, 16, 128)
            IPf[...] = new if i == 0 else IPf[...] + new

    DL[...] = jnp.zeros((8, 2048), F32)

    exchange(0)
    exchange(1)
    ring(0, 0)
    exchange(2)

    with scope("w_first"):
        for h in range(2):
            first_landed(h, 0)
            first(h, 2, -1).start()
            second_out(h, 2, -1)
            first_landed(h, 1)
            first(h, 3, 1).start()
            second_out(h, 3, 1)

    ring(1, 0)

    with scope("norms"):
        landed(SQr.at[0 : N - 1], sqr)
        squares = SQr[0]
        for p in range(1, N):
            squares = squares + SQr[p]
        norms = jnp.sqrt(squares[0:L] + 0.25)
        scales = mag[...] / norms
        for i in range(L):
            SC[i : i + 1, own] = scales[i : i + 1]
        landed(SQr.at[0 : N - 1], sqs)
        SQ[0:L] = scales
        to_col(lambda q: rcopy(SQ, SC.at[:, own], scs, scr, col=q))

    ring(0, 1)

    with scope("psum"):
        landed(PPr.at[0 : N - 1], p1r)
        total = PPr[0].astype(F32)
        for p in range(1, N):
            total = total + PPr[p].astype(F32)
        PSb[...] = total.astype(BF16)
        PD[c] = PSb[...]
        to_col(lambda q: rcopy(PSb, PD.at[c], p2s, p2r, col=q))

    ring(2, 0)

    second_on(1)
    with scope("w_first2"):
        for h in range(2):
            first_landed(h, 2)
            first_landed(h, 3)
            second_out(h, 4, 2)

    ring(1, 1)
    ring(0, 2)

    second_on(2)
    second_on(3)

    ring(2, 1)

    with scope("p_on"):
        landed(PD.at[0 : N - 1], p2r)
        PE[r] = PD[r]
        to_row(lambda p: rcopy(PD.at[p], PE.at[r], pbs, pbr, row=p))

    ring(1, 2)
    second_on(4)
    ring(0, 3)
    ring(2, 2)

    with scope("w_end"):
        for h in range(2):
            for slot, j in offsets:
                second_landed(h, 2, slot, j)
                second_landed(h, 3, slot, j)
        landed(D1r.at[0 : N - 1], scr)
    for i in range(3):
        prepare(i)

    ring(1, 3)
    for i in range(3, L):
        prepare(i)
    ring(0, 4)
    ring_landed(0)
    grads_of(0)
    dots_of(0)
    ring(2, 3)
    grads_of(1)
    dots_of(1)

    with scope("u"):
        landed(PE.at[0 : N - 1], pbr)
        kind = lax.broadcasted_iota(jnp.int32, (256, 128), 0) % 16 // 2
        low = PE[...].reshape(N * 16, 256)
        inner_outer = jnp.zeros((256, 128), F32)
        for i in range(L):
            inner_outer = jnp.where(kind == i, nn(low, grads[i]), inner_outer)
        USb[:, 0:16, :] = inner_outer.astype(BF16).reshape(N, 16, 128)
        USr[r] = USb[r]
        to_row(lambda p: rcopy(USb.at[p], USr.at[r], uss, usr, row=p))

    ring(1, 4)
    ring_landed(1)
    dots_of(2)
    dots_of(3)
    grads_of(2)
    ring(2, 4)
    ring_landed(2)
    dots_of(4)
    dots_of(5)

    with scope("d1send"):
        D1r[c] = DL[:, own]
        to_col(lambda q: rcopy(DL.at[:, pl.ds(aligned(q, 128), 128)], D1r.at[c], d1s, d1r, col=q))
    for i in range(3, L):
        grads_of(i)
    stores = [
        pltpu.make_async_copy(o_in, h_in, out_s.at[0]),
        pltpu.make_async_copy(o_mag, h_mag_grad, out_s.at[1]),
        pltpu.make_async_copy(o_ain, h_ain_grad, out_s.at[2]),
        pltpu.make_async_copy(o_aout, h_aout_grad, out_s.at[3]),
    ]
    stores[0].start()
    with scope("irsend"):
        IRr[c] = IPf[c]
        to_col(lambda q: rcopy(IPf.at[q], IRr.at[c], irs, irr, col=q))

    with scope("d1"):
        landed(D1r.at[0 : N - 1], d1r)
        sub = D1r[0]
        for p in range(1, N):
            sub = sub + D1r[p]
        landed(SQr.at[0 : N - 1], scs)
        SQ[...] = sub
        D2r[r] = sub
        to_row(lambda p: rcopy(SQ, D2r.at[r], d2s, d2r, row=p))

    with scope("us"):
        landed(USr.at[0 : N - 1], usr)
        both = USr[0].astype(F32)
        for p in range(1, N):
            both = both + USr[p].astype(F32)

    with scope("d2"):
        landed(D2r.at[0 : N - 1], d2r)
        dots8 = D2r[0]
        for p in range(1, N):
            dots8 = dots8 + D2r[p]
        dots = dots8[0:L]
        o_mag[...] = dots / norms
        stores[1].start()
        correct = -mag[...] * dots / (norms * norms * norms)
        for i in range(L):
            CR[i : i + 1, own] = correct[i : i + 1]
        landed(D1r.at[0 : N - 1], d1s)
        landed(D2r.at[0 : N - 1], d2s)
        SQ[0:L] = correct
        to_col(lambda q: rcopy(SQ, CR.at[:, own], d3s, d3r, col=q))
        out = jnp.zeros((16, 128), F32)
        kind16 = lax.broadcasted_iota(jnp.int32, (16, 128), 0) // 2
        for i in range(L):
            out = jnp.where(kind16 == i, both[0:16] * scales[i : i + 1] + both[16:32] * correct[i : i + 1], out)
        OGr[r] = out
        to_row(lambda p: rcopy(OGr.at[r], OGr.at[r], ogs, ogr, row=p))

    with scope("ir"):
        landed(IRr.at[0 : N - 1], irr)
        in_sum = IRr[0]
        for p in range(1, N):
            in_sum = in_sum + IRr[p]
        IAr[c] = in_sum
        to_col(lambda q: rcopy(IAr.at[c], IAr.at[c], ias, iar, col=q))

    with scope("d3"):
        landed(D1r.at[0 : N - 1], d3r)
    with scope("term2"):
        for i in range(L):
            second_term = jnp.zeros((64, 128), F32)
            for n in range(NCH):
                cols = pl.ds(n * CH, CH)
                scaled_out = WA[i, 128:160, cols].astype(F32) * CR[i : i + 1, cols]
                high = scaled_out.astype(BF16)
                rest = (scaled_out - high.astype(F32)).astype(BF16)
                second_term += nt(jnp.concatenate([high, rest], axis=0), WM[i, :, cols])
            o_ain[i] = second_term[0:32] + second_term[32:64]

    with scope("og"):
        landed(OGr.at[0 : N - 1], ogr)
        out_all = OGr[...].reshape(N * 16, 128)
        for i in range(L):
            o_aout[i] = exact(collect(i), out_all)
        stores[3].start()

    with scope("ia"):
        landed(IAr.at[0 : N - 1], iar)
        in_all = IAr[...].reshape(N * 16, 128)
        for i in range(L):
            o_ain[i] += exact(collect(i), in_all)
        stores[2].start()

    with scope("drain"):
        for g in range(NG):
            landed(H.at[0 : N - 1, layers(g)], t1s.at[g])
            landed(H.at[0 : N - 1, layers(g)], t2s.at[g])
            for s in range(4):
                right(g, s).wait_send()
                left(g, s).wait_send()
            for n, i in enumerate(hops):
                over(g, n, i).wait_send()
        for h in range(2):
            for n, j in enumerate((0, 0, -1, 1)):
                first(h, n, j).wait_send()
            for slot, j in offsets:
                for n, jb in enumerate((0, 0, -1, 1)):
                    second(h, n, slot, j, jb).wait_send()
        landed(PPr.at[0 : N - 1], p1s)
        landed(USr.at[0 : N - 1], uss)
        landed(D1r.at[0 : N - 1], d3s)
        landed(OGr.at[0 : N - 1], ogs)
        landed(IRr.at[0 : N - 1], irs)
        landed(IAr.at[0 : N - 1], ias)

        landed(PPr.at[0 : N - 1], p2s)
        landed(PPr.at[0 : N - 1], pbs)
        for store in stores:
            store.wait()


def results(a, b, d, e, oa, ob, od, oe, sems):
    copies = [
        pltpu.make_async_copy(have, out, sems.at[n])
        for n, (have, out) in enumerate(((a, oa), (b, ob), (d, od), (e, oe)))
    ]
    for copy in copies:
        copy.start()
    for copy in copies:
        copy.wait()


def body(attn_out, out_cotangent, frozen, adapt_in, adapt_out, magnitude):
    dma = pltpu.SemaphoreType.DMA
    hbm = pl.BlockSpec(memory_space=pltpu.HBM)
    V = pltpu.VMEM
    scratch = [
        V((L, 256, 128), BF16),
        V((L, 256, 128), BF16),
        V((L, 32, 128), BF16),
        V((L, 128), F32),
        V((L, 256, 128), BF16),
        V((L, 32, 128), F32),
        V((L, 32, 128), F32),
        V((L, 128), F32),
        V((N, L, 16, 128), BF16),
        V((L, 256, 2048), BF16),
        V((L, 160, 2048), BF16),
        V((L, 128, 2048), F32),
        V((L, 128, 2048), BF16),
        V((8, 128), F32),
        V((N, 8, 128), F32),
        V((8, 2048), F32),
        V((8, 2048), F32),
        V((N, 16, 256), BF16),
        V((N, 16, 256), BF16),
        V((16, 256), BF16),
        V((N, 16, 256), BF16),
        V((N, 16, 256), BF16),
        V((N, 32, 128), BF16),
        V((N, 32, 128), BF16),
        V((8, 2048), F32),
        V((N, 8, 128), F32),
        V((N, 8, 128), F32),
        V((N, 16, 128), F32),
        V((N, 16, 128), F32),
        V((N, 16, 128), F32),
        V((N, 16, 128), F32),
        dma((6,)), dma((4,)),
        dma((NG,)), dma((NG,)), dma((NG,)), dma((NG,)),
        dma((NG, 4)), dma((NG, 4)), dma((NG, 4)), dma((NG, 4)),
        dma((NG, 8)), dma((NG, 8)),
        dma((2, 5, 4)), dma((2, 5, 4)),
        dma, dma, dma, dma, dma, dma, dma, dma,
        dma, dma, dma, dma,
        dma, dma, dma, dma, dma, dma, dma, dma, dma, dma, dma, dma,
    ]
    shapes = (
        jax.ShapeDtypeStruct((L, 256, 128), BF16),
        jax.ShapeDtypeStruct((L, 32, 128), F32),
        jax.ShapeDtypeStruct((L, 32, 128), F32),
        jax.ShapeDtypeStruct((L, 128), F32),
    )
    found = pl.pallas_call(
        kernel,
        out_shape=shapes,
        in_specs=[hbm] * 6,
        out_specs=(hbm,) * 4,
        scratch_shapes=scratch,
        compiler_params=pltpu.CompilerParams(
            collective_id=0, has_side_effects=True, vmem_limit_bytes=67043328
        ),
        name="dora",
    )(attn_out, out_cotangent, adapt_in, magnitude, frozen, adapt_out)
    return pl.pallas_call(
        results,
        out_shape=shapes,
        in_specs=[pl.BlockSpec(memory_space=pltpu.VMEM)] * 4,
        out_specs=(hbm,) * 4,
        scratch_shapes=[dma((4,))],
        compiler_params=pltpu.CompilerParams(vmem_limit_bytes=67043328),
        name="results",
    )(*found)

def solution(mesh):
    return jax.shard_map(
        body,
        mesh=mesh,
        in_specs=(
            P(None, "col", "row"),
            P(None, "row", "col"),
            P(None, "row", "col"),
            P(None, None, "row"),
            P(None, None, "col"),
            P(None, "col"),
        ),
        out_specs=(
            P(None, "col", "row"),
            P(None, None, "row"),
            P(None, None, "col"),
            P(None, "col"),
        ),
        check_vma=False,
    )
```

time: 489 us -> 84 us (0.17)
  the two profiles are of different devices: /device:TPU:160 before, /device:TPU:1 now
where the time goes in v2:
time: 84 us; the launch traced here: 83.8 us
  Pallas kernels  83.2 us (99%)
    pallas_call x1, Pallas kernels, body(): pl.pallas_call(kernel, out_shape=shapes, in_specs=[hbm] * 6, out_specs=(h...  81.3 us
    pallas_call x1, Pallas kernels, body(): pl.pallas_call(results, out_shape=shapes, in_specs=[pl.BlockSpec(memory_s...  1.9 us

profile of v2, /device:TPU:1, one launch (start us, length us, event | category | flops | bytes accessed | tf_op | source)
XLA Modules:
  0.0 83.8 jit_solution(14808247974592635778)
XLA Ops:
  0.6 81.3 %dora.1 = (bf16[6,256,128]{2,1,0:T(8,128)(2,1)}, f32[6,32,128]{2,1,0:T(8,128)}, f32[6,32,128]{2,1,0:T(8,128)}, f32[6,128]{1,0:T(8,128)}) custom-call(bf16[6,256,128]{2,1,0:T(8,128)(2,1)} %h_acts.1, bf16[6,256,128]{2,1,0:T(8,128)(2,1)} %h_grads.1, bf16[6,32,128]{2,1,0:T(8,128)(2,1)} %h_ain.1, f32[6,128]{1,0:T(8,128)} %h_mag.1, bf16[6,128,128]{2,1,0:T(8,128)(2,1)} %h_frozen.1, ...), custom_call_target="tpu_custom_call" | custom-call | tf_op jit(solution)/shard_map/dora/pallas_call | solution.py:573
  81.9 1.9 %results.1 = (bf16[6,256,128]{2,1,0:T(8,128)(2,1)}, f32[6,32,128]{2,1,0:T(8,128)}, f32[6,32,128]{2,1,0:T(8,128)}, f32[6,128]{1,0:T(8,128)}) custom-call(bf16[6,256,128]{2,1,0:T(8,128)(2,1)} %get-tuple-element.8.a, f32[6,32,128]{2,1,0:T(8,128)} %get-tuple-element.9.b, f32[6,32,128]{2,1,0:T(8,128)} %get-tuple-element.10.d, f32[6,128]{1,0:T(8,128)} %get-tuple-element.11.e), custom_call_target="tpu_custom_call" | custom-call | tf_op jit(solution)/shard_map/results/pallas_call | solution.py:584

commit v3 on v2

--- a/solution.py
+++ b/solution.py
@@ -9,7 +9,6 @@
 
 F32 = jnp.float32
 BF16 = jnp.bfloat16
-HIGH = lax.Precision.HIGHEST
 N = 16
 ZS = 8
 L = 6
@@ -31,10 +30,6 @@
     return lax.dot_general(a, b, (((0,), (0,)), ((), ())), preferred_element_type=F32)
 
 
-def exact(a, b):
-    return lax.dot_general(a, b, (((1,), (0,)), ((), ())), precision=HIGH, preferred_element_type=F32)
-
-
 def aligned(i, n):
     return pl.multiple_of(i * n, n)
 
@@ -43,7 +38,7 @@
     h_acts, h_grads, h_ain, h_mag, h_frozen, h_aout,
     h_in, h_ain_grad, h_aout_grad, h_mag_grad,
     acts, grads, ain, mag, o_in, o_ain, o_aout, o_mag,
-    H, G, WA, MF, WM, SQ, SQr, SC, CR, PPb, PPr, PSb, PD, PE, USb, USr, DL, D1r, D2r, OGr, IPf, IRr, IAr,
+    H, G, WA, MF, WM, SQ, SQx, SQr, SC, CR, PPf, PPx, PPb, PPr, PSb, PD, PE, USb, USr, DL, D1r, D2r, OGr, IPf, IRr, IAr, TMP,
     in_s, out_s, t1s, t1r, t2s, t2r, rs, rr, ls, lr, ds, dr, ws, wr,
     sqs, sqr, scs, scr, p1s, p1r, p2s, p2r, pbs, pbr, uss, usr,
     d1s, d1r, d2s, d2r, d3s, d3r, ogs, ogr, irs, irr, ias, iar,
@@ -51,6 +46,8 @@
     r = lax.axis_index("row")
     c = lax.axis_index("col")
     z, k = r // 2, r % 2
+    slot = k * ZS + z
+    partner = z * 2 + 1 - k
     x, y = c // 4, c % 4
     scope = jax.named_scope
 
@@ -173,13 +170,6 @@
         off = rows % 16 - 2 * i
         return jnp.where((off >= 0) & (off < 2) & (ranks == rows // 16 * 2 + off), 1.0, 0.0).astype(F32)
 
-    back_rows = lax.broadcasted_iota(jnp.int32, (32, 256), 1)
-    back_ranks = lax.broadcasted_iota(jnp.int32, (32, 256), 0)
-
-    def collect(i):
-        off = back_rows % 16 - 2 * i
-        return jnp.where((off >= 0) & (off < 2) & (back_ranks == back_rows // 16 * 2 + off), 1.0, 0.0).astype(F32)
-
     with scope("s02_local"):
         SQ[...] = jnp.zeros((8, 128), F32)
         part = jnp.zeros((256, 256), F32)
@@ -191,12 +181,31 @@
             part += nt(wide, acts[i])
             high = block.astype(BF16)
             inner += nn(wide, high) + nn(wide, (block - high.astype(F32)).astype(BF16))
-        PPb[...] = part.astype(BF16).reshape(N, 16, 256)
+        PPf[...] = part.reshape(N, 16, 256)
         USb[:, 16:32, :] = inner.astype(BF16).reshape(N, 16, 128)
-        SQr[r] = SQ[...]
-        to_row(lambda p: rcopy(SQ, SQr.at[r], sqs, sqr, row=p))
-        PPr[r] = PPb[r]
-        to_row(lambda p: rcopy(PPb.at[p], PPr.at[r], p1s, p1r, row=p))
+        theirs = pl.ds(aligned(1 - k, ZS), ZS)
+        to_partner = [
+            rcopy(SQ, SQx, sqs, sqr.at[0], row=partner),
+            rcopy(PPf.at[theirs], PPx, p1s, p1r.at[0], row=partner),
+        ]
+        for copy in to_partner:
+            copy.start()
+
+    def to_column(make):
+        def step(i, _):
+            make(lax.rem(z + i, ZS)).start()
+            return 0
+        lax.fori_loop(1, ZS, step, 0)
+
+    with scope("pairs"):
+        for copy in to_partner:
+            copy.wait()
+        SQ[...] = SQ[...] + SQx[...]
+        SQr[z] = SQ[...]
+        to_column(lambda q: rcopy(SQ, SQr.at[z], sqs, sqr.at[1], row=q * 2 + k))
+        PPb[...] = (PPf[pl.ds(aligned(k, ZS), ZS)] + PPx[...]).astype(BF16)
+        PPr[z] = PPb[z]
+        to_column(lambda q: rcopy(PPb.at[q], PPr.at[z], p1s, p1r.at[1], row=q * 2 + k))
 
     def exchange(g):
         with scope(f"t2_{g}"):
@@ -218,8 +227,6 @@
     def left(g, s):
         ref = chunk(g, across(s)) if s < 3 else chunk(g, across(s), 1, 1)
         return rcopy(ref, ref, ls.at[g, s], lr.at[g, s], row=across(-1))
-
-    partner = z * 2 + 1 - k
 
     def over(g, n, i):
         ref = chunk(g, across(i))
@@ -278,46 +285,50 @@
             o_in[i] = got.astype(BF16)
             high = low_t.astype(BF16)
             rest = (low_t - high.astype(F32)).astype(BF16)
-            new = exact(spread(i), nn(high, acts[i]) + nn(rest, acts[i])).reshape(N, 16, 128)
-            IPf[...] = new if i == 0 else IPf[...] + new
+            TMP[...] = nn(high, acts[i]) + nn(rest, acts[i])
+            for q in range(2):
+                IPf[pl.ds(2 * i + q, N, stride=16), :] = TMP[pl.ds(q, N, stride=2), :]
 
     DL[...] = jnp.zeros((8, 2048), F32)
+    IPf[...] = jnp.zeros((N * 16, 128), F32)
 
     exchange(0)
     exchange(1)
-    ring(0, 0)
-    exchange(2)
 
     with scope("w_first"):
         for h in range(2):
             first_landed(h, 0)
             first(h, 2, -1).start()
-            second_out(h, 2, -1)
             first_landed(h, 1)
             first(h, 3, 1).start()
-            second_out(h, 3, 1)
-
+
+    ring(0, 0)
+    exchange(2)
+    for h in range(2):
+        second_out(h, 2, -1)
+        second_out(h, 3, 1)
+    second_on(1)
     ring(1, 0)
 
     with scope("norms"):
-        landed(SQr.at[0 : N - 1], sqr)
+        landed(SQr.at[0 : ZS - 1], sqr.at[1])
         squares = SQr[0]
-        for p in range(1, N):
+        for p in range(1, ZS):
             squares = squares + SQr[p]
         norms = jnp.sqrt(squares[0:L] + 0.25)
         scales = mag[...] / norms
         for i in range(L):
             SC[i : i + 1, own] = scales[i : i + 1]
-        landed(SQr.at[0 : N - 1], sqs)
+        landed(SQr.at[0 : ZS - 1], sqs)
         SQ[0:L] = scales
         to_col(lambda q: rcopy(SQ, SC.at[:, own], scs, scr, col=q))
 
     ring(0, 1)
 
     with scope("psum"):
-        landed(PPr.at[0 : N - 1], p1r)
+        landed(PPr.at[0 : ZS - 1], p1r.at[1])
         total = PPr[0].astype(F32)
-        for p in range(1, N):
+        for p in range(1, ZS):
             total = total + PPr[p].astype(F32)
         PSb[...] = total.astype(BF16)
         PD[c] = PSb[...]
@@ -325,7 +336,6 @@
 
     ring(2, 0)
 
-    second_on(1)
     with scope("w_first2"):
         for h in range(2):
             first_landed(h, 2)
@@ -333,43 +343,50 @@
             second_out(h, 4, 2)
 
     ring(1, 1)
-    ring(0, 2)
-
     second_on(2)
     second_on(3)
-
     ring(2, 1)
-
-    with scope("p_on"):
-        landed(PD.at[0 : N - 1], p2r)
-        PE[r] = PD[r]
-        to_row(lambda p: rcopy(PD.at[p], PE.at[r], pbs, pbr, row=p))
-
+    ring(0, 2)
     ring(1, 2)
     second_on(4)
-    ring(0, 3)
     ring(2, 2)
 
     with scope("w_end"):
         for h in range(2):
-            for slot, j in offsets:
-                second_landed(h, 2, slot, j)
-                second_landed(h, 3, slot, j)
+            for place, j in offsets:
+                second_landed(h, 2, place, j)
+                second_landed(h, 3, place, j)
         landed(D1r.at[0 : N - 1], scr)
     for i in range(3):
         prepare(i)
 
-    ring(1, 3)
+    ring(0, 3)
     for i in range(3, L):
         prepare(i)
+    ring(1, 3)
+    ring(2, 3)
+
+    with scope("p_on"):
+        landed(PD.at[0 : N - 1], p2r)
+        PE[slot] = PD[r]
+        to_row(lambda p: rcopy(PD.at[p], PE.at[slot], pbs, pbr, row=p))
+
     ring(0, 4)
+    ring(1, 4)
     ring_landed(0)
-    grads_of(0)
     dots_of(0)
-    ring(2, 3)
-    grads_of(1)
     dots_of(1)
-
+    ring(2, 4)
+    ring_landed(1)
+    dots_of(2)
+    dots_of(3)
+    ring_landed(2)
+    dots_of(4)
+    dots_of(5)
+
+    with scope("d1send"):
+        D1r[c] = DL[:, own]
+        to_col(lambda q: rcopy(DL.at[:, pl.ds(aligned(q, 128), 128)], D1r.at[c], d1s, d1r, col=q))
     with scope("u"):
         landed(PE.at[0 : N - 1], pbr)
         kind = lax.broadcasted_iota(jnp.int32, (256, 128), 0) % 16 // 2
@@ -378,23 +395,23 @@
         for i in range(L):
             inner_outer = jnp.where(kind == i, nn(low, grads[i]), inner_outer)
         USb[:, 0:16, :] = inner_outer.astype(BF16).reshape(N, 16, 128)
-        USr[r] = USb[r]
-        to_row(lambda p: rcopy(USb.at[p], USr.at[r], uss, usr, row=p))
-
-    ring(1, 4)
-    ring_landed(1)
-    dots_of(2)
-    dots_of(3)
-    grads_of(2)
-    ring(2, 4)
-    ring_landed(2)
-    dots_of(4)
-    dots_of(5)
-
-    with scope("d1send"):
-        D1r[c] = DL[:, own]
-        to_col(lambda q: rcopy(DL.at[:, pl.ds(aligned(q, 128), 128)], D1r.at[c], d1s, d1r, col=q))
-    for i in range(3, L):
+        USr[slot] = USb[slot]
+        to_row(lambda p: rcopy(USb.at[lax.rem(p, 2) * ZS + p // 2], USr.at[slot], uss, usr, row=p))
+
+    for i in range(4):
+        grads_of(i)
+
+    with scope("d1"):
+        landed(D1r.at[0 : N - 1], d1r)
+        sub = D1r[0]
+        for p in range(1, N):
+            sub = sub + D1r[p]
+        landed(D1r.at[0 : N - 1], scs)
+        SQ[...] = sub
+        D2r[r] = sub
+        to_row(lambda p: rcopy(SQ, D2r.at[r], d2s, d2r, row=p))
+
+    for i in range(4, L):
         grads_of(i)
     stores = [
         pltpu.make_async_copy(o_in, h_in, out_s.at[0]),
@@ -404,83 +421,10 @@
     ]
     stores[0].start()
     with scope("irsend"):
-        IRr[c] = IPf[c]
-        to_col(lambda q: rcopy(IPf.at[q], IRr.at[c], irs, irr, col=q))
-
-    with scope("d1"):
-        landed(D1r.at[0 : N - 1], d1r)
-        sub = D1r[0]
-        for p in range(1, N):
-            sub = sub + D1r[p]
-        landed(SQr.at[0 : N - 1], scs)
-        SQ[...] = sub
-        D2r[r] = sub
-        to_row(lambda p: rcopy(SQ, D2r.at[r], d2s, d2r, row=p))
-
-    with scope("us"):
-        landed(USr.at[0 : N - 1], usr)
-        both = USr[0].astype(F32)
-        for p in range(1, N):
-            both = both + USr[p].astype(F32)
-
-    with scope("d2"):
-        landed(D2r.at[0 : N - 1], d2r)
-        dots8 = D2r[0]
-        for p in range(1, N):
-            dots8 = dots8 + D2r[p]
-        dots = dots8[0:L]
-        o_mag[...] = dots / norms
-        stores[1].start()
-        correct = -mag[...] * dots / (norms * norms * norms)
-        for i in range(L):
-            CR[i : i + 1, own] = correct[i : i + 1]
-        landed(D1r.at[0 : N - 1], d1s)
-        landed(D2r.at[0 : N - 1], d2s)
-        SQ[0:L] = correct
-        to_col(lambda q: rcopy(SQ, CR.at[:, own], d3s, d3r, col=q))
-        out = jnp.zeros((16, 128), F32)
-        kind16 = lax.broadcasted_iota(jnp.int32, (16, 128), 0) // 2
-        for i in range(L):
-            out = jnp.where(kind16 == i, both[0:16] * scales[i : i + 1] + both[16:32] * correct[i : i + 1], out)
-        OGr[r] = out
-        to_row(lambda p: rcopy(OGr.at[r], OGr.at[r], ogs, ogr, row=p))
-
-    with scope("ir"):
-        landed(IRr.at[0 : N - 1], irr)
-        in_sum = IRr[0]
-        for p in range(1, N):
-            in_sum = in_sum + IRr[p]
-        IAr[c] = in_sum
-        to_col(lambda q: rcopy(IAr.at[c], IAr.at[c], ias, iar, col=q))
-
-    with scope("d3"):
-        landed(D1r.at[0 : N - 1], d3r)
-    with scope("term2"):
-        for i in range(L):
-            second_term = jnp.zeros((64, 128), F32)
-            for n in range(NCH):
-                cols = pl.ds(n * CH, CH)
-                scaled_out = WA[i, 128:160, cols].astype(F32) * CR[i : i + 1, cols]
-                high = scaled_out.astype(BF16)
-                rest = (scaled_out - high.astype(F32)).astype(BF16)
-                second_term += nt(jnp.concatenate([high, rest], axis=0), WM[i, :, cols])
-            o_ain[i] = second_term[0:32] + second_term[32:64]
-
-    with scope("og"):
-        landed(OGr.at[0 : N - 1], ogr)
-        out_all = OGr[...].reshape(N * 16, 128)
-        for i in range(L):
-            o_aout[i] = exact(collect(i), out_all)
-        stores[3].start()
-
-    with scope("ia"):
-        landed(IAr.at[0 : N - 1], iar)
-        in_all = IAr[...].reshape(N * 16, 128)
-        for i in range(L):
-            o_ain[i] += exact(collect(i), in_all)
-        stores[2].start()
-
-    with scope("drain"):
+        IRr[c] = IPf[pl.ds(aligned(c, 16), 16), :]
+        to_col(lambda q: rcopy(IPf.at[pl.ds(aligned(q, 16), 16), :], IRr.at[c], irs, irr, col=q))
+
+    with scope("drain0"):
         for g in range(NG):
             landed(H.at[0 : N - 1, layers(g)], t1s.at[g])
             landed(H.at[0 : N - 1, layers(g)], t2s.at[g])
@@ -492,30 +436,100 @@
         for h in range(2):
             for n, j in enumerate((0, 0, -1, 1)):
                 first(h, n, j).wait_send()
-            for slot, j in offsets:
+            for place, j in offsets:
                 for n, jb in enumerate((0, 0, -1, 1)):
-                    second(h, n, slot, j, jb).wait_send()
-        landed(PPr.at[0 : N - 1], p1s)
+                    second(h, n, place, j, jb).wait_send()
+        landed(PPr.at[0 : ZS - 1], p1s)
+        landed(PD.at[0 : N - 1], p2s)
+        landed(PD.at[0 : N - 1], pbs)
+
+    with scope("us"):
+        landed(USr.at[0 : N - 1], usr)
+        both = USr[0].astype(F32)
+        for p in range(1, N):
+            both = both + USr[p].astype(F32)
+
+    with scope("d2"):
+        landed(D2r.at[0 : N - 1], d2r)
+        dots8 = D2r[0]
+        for p in range(1, N):
+            dots8 = dots8 + D2r[p]
+        dots = dots8[0:L]
+        o_mag[...] = dots / norms
+        stores[1].start()
+        correct = -mag[...] * dots / (norms * norms * norms)
+        for i in range(L):
+            CR[i : i + 1, own] = correct[i : i + 1]
+        landed(D1r.at[0 : N - 1], d1s)
+        landed(D2r.at[0 : N - 1], d2s)
+        SQ[0:L] = correct
+        to_col(lambda q: rcopy(SQ, CR.at[:, own], d3s, d3r, col=q))
+        out = jnp.zeros((16, 128), F32)
+        kind16 = lax.broadcasted_iota(jnp.int32, (16, 128), 0) // 2
+        for i in range(L):
+            out = jnp.where(kind16 == i, both[0:16] * scales[i : i + 1] + both[16:32] * correct[i : i + 1], out)
+        OGr[pl.ds(aligned(slot, 16), 16), :] = out
+        ranks_out = OGr.at[pl.ds(aligned(slot, 16), 16), :]
+        to_row(lambda p: rcopy(ranks_out, ranks_out, ogs, ogr, row=p))
+
+    with scope("ir"):
+        landed(IRr.at[0 : N - 1], irr)
+        in_sum = IRr[0]
+        for p in range(1, N):
+            in_sum = in_sum + IRr[p]
+        IAr[pl.ds(aligned(c, 16), 16), :] = in_sum
+        block = IAr.at[pl.ds(aligned(c, 16), 16), :]
+        to_col(lambda q: rcopy(block, block, ias, iar, col=q))
+
+    with scope("d3"):
+        landed(D1r.at[0 : N - 1], d3r)
+    with scope("term2"):
+        for i in range(L):
+            second_term = jnp.zeros((128, 64), F32)
+            for n in range(NCH):
+                cols = pl.ds(n * CH, CH)
+                scaled_out = WA[i, 128:160, cols].astype(F32) * CR[i : i + 1, cols]
+                high = scaled_out.astype(BF16)
+                rest = (scaled_out - high.astype(F32)).astype(BF16)
+                second_term += nt(WM[i, :, cols], jnp.concatenate([high, rest], axis=0))
+            o_ain[i] = jnp.transpose(second_term[:, 0:32] + second_term[:, 32:64])
+
+    with scope("og"):
+        landed(OGr.at[0 : 240, :], ogr)
+        for i in range(L):
+            for q in range(2):
+                o_aout[i, pl.ds(q, N, stride=2), :] = OGr[pl.ds(2 * i + q, N, stride=16), :]
+        stores[3].start()
+
+    with scope("ia"):
+        landed(IAr.at[0 : 240, :], iar)
+        for i in range(L):
+            for q in range(2):
+                o_ain[i, pl.ds(q, N, stride=2), :] += IAr[pl.ds(2 * i + q, N, stride=16), :]
+        stores[2].start()
+
+    with scope("drain"):
         landed(USr.at[0 : N - 1], uss)
         landed(D1r.at[0 : N - 1], d3s)
-        landed(OGr.at[0 : N - 1], ogs)
+        landed(OGr.at[0 : 240, :], ogs)
         landed(IRr.at[0 : N - 1], irs)
-        landed(IAr.at[0 : N - 1], ias)
-
-        landed(PPr.at[0 : N - 1], p2s)
-        landed(PPr.at[0 : N - 1], pbs)
+        landed(IAr.at[0 : 240, :], ias)
         for store in stores:
             store.wait()
 
 
-def results(a, b, d, e, oa, ob, od, oe, sems):
-    copies = [
-        pltpu.make_async_copy(have, out, sems.at[n])
-        for n, (have, out) in enumerate(((a, oa), (b, ob), (d, od), (e, oe)))
-    ]
-    for copy in copies:
+def results(a, b, d, e, oa, ob, od, oe, va, vb, vd, ve, sems):
+    into = []
+    away = []
+    for n, (have, held, out) in enumerate(((a, va, oa), (b, vb, ob), (d, vd, od), (e, ve, oe))):
+        into.append(pltpu.make_async_copy(have, held, sems.at[n]))
+        away.append(pltpu.make_async_copy(held, out, sems.at[4 + n]))
+    for copy in into:
         copy.start()
-    for copy in copies:
+    for n in range(4):
+        into[n].wait()
+        away[n].start()
+    for copy in away:
         copy.wait()
 
 
@@ -538,11 +552,14 @@
         V((L, 128, 2048), F32),
         V((L, 128, 2048), BF16),
         V((8, 128), F32),
-        V((N, 8, 128), F32),
+        V((8, 128), F32),
+        V((ZS, 8, 128), F32),
         V((8, 2048), F32),
         V((8, 2048), F32),
-        V((N, 16, 256), BF16),
-        V((N, 16, 256), BF16),
+        V((N, 16, 256), F32),
+        V((ZS, 16, 256), F32),
+        V((ZS, 16, 256), BF16),
+        V((ZS, 16, 256), BF16),
         V((16, 256), BF16),
         V((N, 16, 256), BF16),
         V((N, 16, 256), BF16),
@@ -551,16 +568,17 @@
         V((8, 2048), F32),
         V((N, 8, 128), F32),
         V((N, 8, 128), F32),
+        V((N * 16, 128), F32),
+        V((N * 16, 128), F32),
         V((N, 16, 128), F32),
-        V((N, 16, 128), F32),
-        V((N, 16, 128), F32),
-        V((N, 16, 128), F32),
+        V((N * 16, 128), F32),
+        V((32, 128), F32),
         dma((6,)), dma((4,)),
         dma((NG,)), dma((NG,)), dma((NG,)), dma((NG,)),
         dma((NG, 4)), dma((NG, 4)), dma((NG, 4)), dma((NG, 4)),
         dma((NG, 8)), dma((NG, 8)),
         dma((2, 5, 4)), dma((2, 5, 4)),
-        dma, dma, dma, dma, dma, dma, dma, dma,
+        dma, dma((2,)), dma, dma, dma, dma((2,)), dma, dma,
         dma, dma, dma, dma,
         dma, dma, dma, dma, dma, dma, dma, dma, dma, dma, dma, dma,
     ]
@@ -584,9 +602,9 @@
     return pl.pallas_call(
         results,
         out_shape=shapes,
-        in_specs=[pl.BlockSpec(memory_space=pltpu.VMEM)] * 4,
+        in_specs=[hbm] * 4,
         out_specs=(hbm,) * 4,
-        scratch_shapes=[dma((4,))],
+        scratch_shapes=[V(shape.shape, shape.dtype) for shape in shapes] + [dma((8,))],
         compiler_params=pltpu.CompilerParams(vmem_limit_bytes=67043328),
         name="results",
     )(*found)

time: 84 us -> 79.1 us (0.942)
  Pallas kernels: 83.2 us -> 78.3 us
    pallas_call x1, Pallas kernels: 81.3 us -> 76.5 us  [body(): pl.pallas_call(kernel, out_shape=shapes, in_specs=[hbm] * 6, out_specs=(h...]
where the time goes in v3:
time: 79.1 us; the launch traced here: 79 us
  Pallas kernels  78.3 us (99%)
    pallas_call x1, Pallas kernels, body(): pl.pallas_call(kernel, out_shape=shapes, in_specs=[hbm] * 6, out_specs=(h...  76.5 us
    pallas_call x1, Pallas kernels, body(): pl.pallas_call(results, out_shape=shapes, in_specs=[hbm] * 4, out_specs=(...  1.87 us

profile of v3, /device:TPU:1, one launch (start us, length us, event | category | flops | bytes accessed | tf_op | source)
XLA Modules:
  0.0 79.0 jit_solution(641131995405023223)
XLA Ops:
  0.6 76.5 %dora.1 = (bf16[6,256,128]{2,1,0:T(8,128)(2,1)}, f32[6,32,128]{2,1,0:T(8,128)}, f32[6,32,128]{2,1,0:T(8,128)}, f32[6,128]{1,0:T(8,128)}) custom-call(bf16[6,256,128]{2,1,0:T(8,128)(2,1)} %h_acts.1, bf16[6,256,128]{2,1,0:T(8,128)(2,1)} %h_grads.1, bf16[6,32,128]{2,1,0:T(8,128)(2,1)} %h_ain.1, f32[6,128]{1,0:T(8,128)} %h_mag.1, bf16[6,128,128]{2,1,0:T(8,128)(2,1)} %h_frozen.1, ...), custom_call_target="tpu_custom_call" | custom-call | tf_op jit(solution)/shard_map/dora/pallas_call | solution.py:591
  77.1 1.9 %results.1 = (bf16[6,256,128]{2,1,0:T(8,128)(2,1)}, f32[6,32,128]{2,1,0:T(8,128)}, f32[6,32,128]{2,1,0:T(8,128)}, f32[6,128]{1,0:T(8,128)}) custom-call(bf16[6,256,128]{2,1,0:T(8,128)(2,1)} %get-tuple-element.8.a, f32[6,32,128]{2,1,0:T(8,128)} %get-tuple-element.9.b, f32[6,32,128]{2,1,0:T(8,128)} %get-tuple-element.10.d, f32[6,128]{1,0:T(8,128)} %get-tuple-element.11.e), custom_call_target="tpu_custom_call" | custom-call | tf_op jit(solution)/shard_map/results/pallas_call | solution.py:602

commit v4 on v3

--- a/solution.py
+++ b/solution.py
@@ -71,6 +71,14 @@
             make(lax.rem(c + i, N)).start()
             return 0
         lax.fori_loop(1, N, step, 0)
+
+    def quick_row(make):
+        for i in (8, 7, 9, 6, 10, 5, 11, 4, 12, 3, 13, 2, 14, 1, 15):
+            make(lax.rem(r + i, N)).start()
+
+    def quick_col(make):
+        for i in (10, 9, 11, 6, 14, 8, 2, 5, 7, 13, 15, 4, 12, 1, 3):
+            make(lax.rem(x + i // 4, 4) * 4 + lax.rem(y + i % 4, 4)).start()
 
     own = pl.ds(aligned(c, 128), 128)
     mine = pl.ds(aligned(r, 16), 16)
@@ -317,6 +325,7 @@
             squares = squares + SQr[p]
         norms = jnp.sqrt(squares[0:L] + 0.25)
         scales = mag[...] / norms
+        minus = -mag[...] / (norms * norms * norms)
         for i in range(L):
             SC[i : i + 1, own] = scales[i : i + 1]
         landed(SQr.at[0 : ZS - 1], sqs)
@@ -386,7 +395,10 @@
 
     with scope("d1send"):
         D1r[c] = DL[:, own]
-        to_col(lambda q: rcopy(DL.at[:, pl.ds(aligned(q, 128), 128)], D1r.at[c], d1s, d1r, col=q))
+        quick_col(lambda q: rcopy(DL.at[:, pl.ds(aligned(q, 128), 128)], D1r.at[c], d1s, d1r, col=q))
+    for i in range(2):
+        grads_of(i)
+
     with scope("u"):
         landed(PE.at[0 : N - 1], pbr)
         kind = lax.broadcasted_iota(jnp.int32, (256, 128), 0) % 16 // 2
@@ -398,7 +410,7 @@
         USr[slot] = USb[slot]
         to_row(lambda p: rcopy(USb.at[lax.rem(p, 2) * ZS + p // 2], USr.at[slot], uss, usr, row=p))
 
-    for i in range(4):
+    for i in range(2, 4):
         grads_of(i)
 
     with scope("d1"):
@@ -409,7 +421,7 @@
         landed(D1r.at[0 : N - 1], scs)
         SQ[...] = sub
         D2r[r] = sub
-        to_row(lambda p: rcopy(SQ, D2r.at[r], d2s, d2r, row=p))
+        quick_row(lambda p: rcopy(SQ, D2r.at[r], d2s, d2r, row=p))
 
     for i in range(4, L):
         grads_of(i)
@@ -457,13 +469,13 @@
         dots = dots8[0:L]
         o_mag[...] = dots / norms
         stores[1].start()
-        correct = -mag[...] * dots / (norms * norms * norms)
+        correct = minus * dots
         for i in range(L):
             CR[i : i + 1, own] = correct[i : i + 1]
         landed(D1r.at[0 : N - 1], d1s)
         landed(D2r.at[0 : N - 1], d2s)
         SQ[0:L] = correct
-        to_col(lambda q: rcopy(SQ, CR.at[:, own], d3s, d3r, col=q))
+        quick_col(lambda q: rcopy(SQ, CR.at[:, own], d3s, d3r, col=q))
         out = jnp.zeros((16, 128), F32)
         kind16 = lax.broadcasted_iota(jnp.int32, (16, 128), 0) // 2
         for i in range(L):
@@ -485,14 +497,12 @@
         landed(D1r.at[0 : N - 1], d3r)
     with scope("term2"):
         for i in range(L):
-            second_term = jnp.zeros((128, 64), F32)
+            second_term = jnp.zeros((128, 32), F32)
             for n in range(NCH):
                 cols = pl.ds(n * CH, CH)
-                scaled_out = WA[i, 128:160, cols].astype(F32) * CR[i : i + 1, cols]
-                high = scaled_out.astype(BF16)
-                rest = (scaled_out - high.astype(F32)).astype(BF16)
-                second_term += nt(WM[i, :, cols], jnp.concatenate([high, rest], axis=0))
-            o_ain[i] = jnp.transpose(second_term[:, 0:32] + second_term[:, 32:64])
+                scaled_out = (WA[i, 128:160, cols].astype(F32) * CR[i : i + 1, cols]).astype(BF16)
+                second_term += nt(WM[i, 0:128, cols], scaled_out)
+            o_ain[i] = jnp.transpose(second_term)
 
     with scope("og"):
         landed(OGr.at[0 : 240, :], ogr)

time: 79.1 us -> 78.4 us (level)
  no operation moved by 1% of the time
where the time goes in v4:
time: 78.4 us; the launch traced here: 78.2 us
  Pallas kernels  77.6 us (99%)
    pallas_call x1, Pallas kernels, body(): pl.pallas_call(kernel, out_shape=shapes, in_specs=[hbm] * 6, out_specs=(h...  75.7 us
    pallas_call x1, Pallas kernels, body(): pl.pallas_call(results, out_shape=shapes, in_specs=[hbm] * 4, out_specs=(...  1.87 us

profile of v4, /device:TPU:1, one launch (start us, length us, event | category | flops | bytes accessed | tf_op | source)
XLA Modules:
  0.0 78.2 jit_solution(4080862987231149222)
XLA Ops:
  0.6 75.7 %dora.1 = (bf16[6,256,128]{2,1,0:T(8,128)(2,1)}, f32[6,32,128]{2,1,0:T(8,128)}, f32[6,32,128]{2,1,0:T(8,128)}, f32[6,128]{1,0:T(8,128)}) custom-call(bf16[6,256,128]{2,1,0:T(8,128)(2,1)} %h_acts.1, bf16[6,256,128]{2,1,0:T(8,128)(2,1)} %h_grads.1, bf16[6,32,128]{2,1,0:T(8,128)(2,1)} %h_ain.1, f32[6,128]{1,0:T(8,128)} %h_mag.1, bf16[6,128,128]{2,1,0:T(8,128)(2,1)} %h_frozen.1, ...), custom_call_target="tpu_custom_call" | custom-call | tf_op jit(solution)/shard_map/dora/pallas_call | solution.py:601
  76.4 1.9 %results.1 = (bf16[6,256,128]{2,1,0:T(8,128)(2,1)}, f32[6,32,128]{2,1,0:T(8,128)}, f32[6,32,128]{2,1,0:T(8,128)}, f32[6,128]{1,0:T(8,128)}) custom-call(bf16[6,256,128]{2,1,0:T(8,128)(2,1)} %get-tuple-element.8.a, f32[6,32,128]{2,1,0:T(8,128)} %get-tuple-element.9.b, f32[6,32,128]{2,1,0:T(8,128)} %get-tuple-element.10.d, f32[6,128]{1,0:T(8,128)} %get-tuple-element.11.e), custom_call_target="tpu_custom_call" | custom-call | tf_op jit(solution)/shard_map/results/pallas_call | solution.py:612

commit v5 on v4

--- a/solution.py
+++ b/solution.py
@@ -105,9 +105,7 @@
         lax.fori_loop(1, N, greet, 0)
         for load in loads:
             load.start()
-        for load in loads:
-            load.wait()
-        H[r] = grads[:, mine, :]
+        loads[0].wait()
         pl.semaphore_wait(barrier, 2 * (N - 1))
 
     with scope("s01_t1send"):
@@ -115,6 +113,10 @@
             to_row(lambda p, g=g: rcopy(
                 grads.at[layers(g), pl.ds(aligned(p, 16), 16), :], H.at[r, layers(g)],
                 t1s.at[g], t1r.at[g], row=p))
+
+    for load in loads[1:]:
+        load.wait()
+    H[r] = grads[:, mine, :]
 
     def place_of(h, a, b):
         return 4 * b + a if h == 0 else 4 * a + b
@@ -237,10 +239,11 @@
         return rcopy(ref, ref, ls.at[g, s], lr.at[g, s], row=across(-1))
 
     def over(g, n, i):
-        ref = chunk(g, across(i))
+        ref = chunk(g, across(i), *parts[n])
         return rcopy(ref, ref, ds.at[g, n], dr.at[g, n], row=partner)
 
-    hops = (0, -1, -2, -3, 1, 2, 3, 4)
+    hops = (0, -1, -2, -3, 1, 2, 3, 4, 4)
+    parts = ((GL, 0),) * 7 + ((1, 0), (1, 1))
 
     def ring(g, s):
         with scope(f"r{g}{s}"):
@@ -258,13 +261,14 @@
                 over(g, 3 + s, s).start()
             else:
                 landed(chunk(g, across(4), 1, 0), rr.at[g, 3])
+                over(g, 7, 4).start()
                 landed(chunk(g, across(4), 1, 1), lr.at[g, 3])
-                over(g, 7, 4).start()
+                over(g, 8, 4).start()
 
     def ring_landed(g):
         with scope(f"r{g}_landed"):
             for n, i in enumerate(hops):
-                landed(chunk(g, lax.rem(z + i + ZS, ZS) * 2 + 1 - k), dr.at[g, n])
+                landed(chunk(g, lax.rem(z + i + ZS, ZS) * 2 + 1 - k, *parts[n]), dr.at[g, n])
 
     def prepare(i):
         with scope(f"prep{i}"):
@@ -434,7 +438,7 @@
     stores[0].start()
     with scope("irsend"):
         IRr[c] = IPf[pl.ds(aligned(c, 16), 16), :]
-        to_col(lambda q: rcopy(IPf.at[pl.ds(aligned(q, 16), 16), :], IRr.at[c], irs, irr, col=q))
+        quick_col(lambda q: rcopy(IPf.at[pl.ds(aligned(q, 16), 16), :], IRr.at[c], irs, irr, col=q))
 
     with scope("drain0"):
         for g in range(NG):
@@ -482,7 +486,7 @@
             out = jnp.where(kind16 == i, both[0:16] * scales[i : i + 1] + both[16:32] * correct[i : i + 1], out)
         OGr[pl.ds(aligned(slot, 16), 16), :] = out
         ranks_out = OGr.at[pl.ds(aligned(slot, 16), 16), :]
-        to_row(lambda p: rcopy(ranks_out, ranks_out, ogs, ogr, row=p))
+        quick_row(lambda p: rcopy(ranks_out, ranks_out, ogs, ogr, row=p))
 
     with scope("ir"):
         landed(IRr.at[0 : N - 1], irr)
@@ -491,7 +495,7 @@
             in_sum = in_sum + IRr[p]
         IAr[pl.ds(aligned(c, 16), 16), :] = in_sum
         block = IAr.at[pl.ds(aligned(c, 16), 16), :]
-        to_col(lambda q: rcopy(block, block, ias, iar, col=q))
+        quick_col(lambda q: rcopy(block, block, ias, iar, col=q))
 
     with scope("d3"):
         landed(D1r.at[0 : N - 1], d3r)
@@ -586,7 +590,7 @@
         dma((6,)), dma((4,)),
         dma((NG,)), dma((NG,)), dma((NG,)), dma((NG,)),
         dma((NG, 4)), dma((NG, 4)), dma((NG, 4)), dma((NG, 4)),
-        dma((NG, 8)), dma((NG, 8)),
+        dma((NG, 9)), dma((NG, 9)),
         dma((2, 5, 4)), dma((2, 5, 4)),
         dma, dma((2,)), dma, dma, dma, dma((2,)), dma, dma,
         dma, dma, dma, dma,

time: 78.4 us -> 78.2 us (level)
  no operation moved by 1% of the time
where the time goes in v5:
time: 78.2 us; the launch traced here: 78.1 us
  Pallas kernels  77.4 us (99%)
    pallas_call x1, Pallas kernels, body(): pl.pallas_call(kernel, out_shape=shapes, in_specs=[hbm] * 6, out_specs=(h...  75.5 us
    pallas_call x1, Pallas kernels, body(): pl.pallas_call(results, out_shape=shapes, in_specs=[hbm] * 4, out_specs=(...  1.87 us

profile of v5, /device:TPU:1, one launch (start us, length us, event | category | flops | bytes accessed | tf_op | source)
XLA Modules:
  0.0 78.1 jit_solution(2110003988819788730)
XLA Ops:
  0.6 75.5 %dora.1 = (bf16[6,256,128]{2,1,0:T(8,128)(2,1)}, f32[6,32,128]{2,1,0:T(8,128)}, f32[6,32,128]{2,1,0:T(8,128)}, f32[6,128]{1,0:T(8,128)}) custom-call(bf16[6,256,128]{2,1,0:T(8,128)(2,1)} %h_acts.1, bf16[6,256,128]{2,1,0:T(8,128)(2,1)} %h_grads.1, bf16[6,32,128]{2,1,0:T(8,128)(2,1)} %h_ain.1, f32[6,128]{1,0:T(8,128)} %h_mag.1, bf16[6,128,128]{2,1,0:T(8,128)(2,1)} %h_frozen.1, ...), custom_call_target="tpu_custom_call" | custom-call | tf_op jit(solution)/shard_map/dora/pallas_call | solution.py:605
  76.2 1.9 %results.1 = (bf16[6,256,128]{2,1,0:T(8,128)(2,1)}, f32[6,32,128]{2,1,0:T(8,128)}, f32[6,32,128]{2,1,0:T(8,128)}, f32[6,128]{1,0:T(8,128)}) custom-call(bf16[6,256,128]{2,1,0:T(8,128)(2,1)} %get-tuple-element.8.a, f32[6,32,128]{2,1,0:T(8,128)} %get-tuple-element.9.b, f32[6,32,128]{2,1,0:T(8,128)} %get-tuple-element.10.d, f32[6,128]{1,0:T(8,128)} %get-tuple-element.11.e), custom_call_target="tpu_custom_call" | custom-call | tf_op jit(solution)/shard_map/results/pallas_call | solution.py:616
